TPU v7x, 32 devices: a 4x4x1 block of a 4x4x8 slice. The times are simulated.
32 devices in a mesh: stage: 1 (over z), dp: 4 (over y), fsdp: 4 (over x), tp: 2 (over core).
Axes of the slice: x: 4, y: 4, z: 1, core: 2. Of those that a mesh axis runs over, the one named last changes fastest.
The devices are a block of a 4x4x8 slice.
Arguments:
- weights: float32 [4, 512, 16384], P('stage', ('fsdp', 'dp'), 'tp')
- momenta: float32 [4, 512, 16384], P('stage', ('fsdp', 'dp'), 'tp')
- gradients: bfloat16 [4, 4, 512, 16384], P(('stage', 'dp'), None, 'fsdp', 'tp')
Outputs:
- output 1: float32 [4, 512, 16384], P('stage', ('fsdp', 'dp'), 'tp')
- output 2: float32 [4, 512, 16384], P('stage', ('fsdp', 'dp'), 'tp')
All inputs are finite; a program needn't handle non-finite values.
Results may differ from a plain program's by a relative error of at most 0.02.
Values are sent between devices in bfloat16 or wider.
A program may use at most 768 MiB of HBM per device.

v0:
```python
import math
import jax
import jax.numpy as jnp
from jax import lax
from jax.sharding import PartitionSpec as P, NamedSharding

MOMENTUM = 0.95
LEARN_RATE = 0.1
WEIGHT_DECAY = 0.1
COEF_A = 3.4445
COEF_B = -4.7750
COEF_C = 2.0315
NORM_EPS = 1e-7
NS_STEPS = 5
ROW_AXES = ('fsdp', 'dp')
GROUP_AXES = ('dp', 'fsdp', 'tp')


def gather_rows(x_blk):
    x_mid = lax.all_gather(x_blk, 'dp', axis=1, tiled=True)
    return lax.all_gather(x_mid, 'fsdp', axis=1, tiled=True)


def solution(mesh):
    mat_spec = P('stage', ROW_AXES, 'tp')
    grad_spec = P(('stage', 'dp'), None, 'fsdp', 'tp')
    tp_size = mesh.shape['tp']

    def local_step(w_blk, m_blk, g_blk):
        g_sum = lax.psum_scatter(g_blk[0].astype(jnp.float32), 'dp', scatter_dimension=1, tiled=True)
        m_new = MOMENTUM * m_blk + g_sum
        x_zero = g_sum + MOMENTUM * m_new
        sq_sum = lax.psum(jnp.sum(x_zero * x_zero, axis=(1, 2)), GROUP_AXES)
        norm_val = jnp.sqrt(sq_sum)[:, None, None]
        x_blk = (x_zero / (norm_val + NORM_EPS)).astype(jnp.bfloat16)
        for step_idx in range(NS_STEPS):
            x_cols = gather_rows(x_blk)
            part_gram = jnp.einsum('kin,kjn->kij', x_blk, x_cols, preferred_element_type=jnp.float32)
            gram_blk = lax.psum_scatter(part_gram, 'tp', scatter_dimension=2, tiled=True).astype(jnp.bfloat16)
            gram_rows = lax.all_gather(gram_blk, 'tp', axis=2, tiled=True)
            gram_cols = gather_rows(gram_blk)
            sq_blk = jnp.einsum('kij,kjl->kil', gram_rows, gram_cols, preferred_element_type=jnp.float32).astype(jnp.bfloat16)
            poly_blk = (COEF_B * gram_blk.astype(jnp.float32) + COEF_C * sq_blk.astype(jnp.float32)).astype(jnp.bfloat16)
            poly_rows = lax.all_gather(poly_blk, 'tp', axis=2, tiled=True)
            product = jnp.einsum('kij,kjn->kin', poly_rows, x_cols, preferred_element_type=jnp.float32)
            x_blk = (COEF_A * x_blk.astype(jnp.float32) + product).astype(jnp.bfloat16)
        col_count = x_blk.shape[2] * tp_size
        update_scale = LEARN_RATE * 0.2 * math.sqrt(col_count)
        decay_factor = 1.0 - LEARN_RATE * WEIGHT_DECAY
        w_new = decay_factor * w_blk - update_scale * x_blk.astype(jnp.float32)
        return w_new, m_new

    return jax.shard_map(local_step, mesh=mesh, in_specs=(mat_spec, mat_spec, grad_spec), out_specs=(mat_spec, mat_spec), check_vma=False)
```

profile of v0, /device:TPU:97, one launch (start us, length us, event | category | flops | bytes accessed | tf_op | source)
XLA Modules:
  0.0 2522.9 jit_solution(1038243928037098748)
XLA Ops:
  18.7 149.2 %reduce-scatter.7.cloned.1.call-done = f32[4,32,8192]{2,1,0:T(8,128)} async-done(((f32[4,128,8192]{2,1,0:T(8,128)}), f32[4,32,8192]{2,1,0:T(8,128)}) %reduce-scatter.7.cloned.1.call-update) | async-done | bytes 4194320 | tf_op jit(solution)/shard_map/reduce_scatter | solution.py:30
  174.2 45.1 %psum.7 = f32[4]{0:T(128)S(1)} all-reduce(f32[4]{0:T(128)S(1)} %get-tuple-element.2), channel_id=1, replica_groups=mesh['stage'=1,'dp'=4,'fsdp'=4,'tp'=2] {'dp','fsdp','tp'}, use_global_device_ids=true, to_apply=%region_2.0 | all-reduce | flops 4 | bytes 32 | tf_op jit(solution)/shard_map/psum | solution.py:33
  224.9 78.7 %all-gather.16.cloned.1.call-done = bf16[4,128,8192]{2,1,0:T(8,128)(2,1)} async-done(((bf16[4,32,8192]{2,1,0:T(8,128)(2,1)}), bf16[4,128,8192]{2,1,0:T(8,128)(2,1)}) %all-gather.16.cloned.1.call-update) | async-done | bytes 8388624 | tf_op jit(solution)/shard_map/all_gather | solution.py:20
  303.7 294.1 %all-gather.18.cloned.1.call-done = bf16[4,512,8192]{2,1,0:T(8,128)(2,1)} async-done(((bf16[4,128,8192]{2,1,0:T(8,128)(2,1)}), bf16[4,512,8192]{2,1,0:T(8,128)(2,1)}) %all-gather.18.cloned.1.call-update) | async-done | bytes 33554448 | tf_op jit(solution)/shard_map/all_gather | solution.py:21
  597.8 15.9 fusion.28
  638.9 17.8 all-gather.20.cloned.1.call-done
  663.1 17.7 fusion
  680.9 81.0 %all-gather.22.cloned.1.call-done = bf16[4,128,8192]{2,1,0:T(8,128)(2,1)} async-done(((bf16[4,32,8192]{2,1,0:T(8,128)(2,1)}), bf16[4,128,8192]{2,1,0:T(8,128)(2,1)}) %all-gather.22.cloned.1.call-update) | async-done | bytes 8388624 | tf_op jit(solution)/shard_map/all_gather | solution.py:20
  762.0 294.1 %all-gather.24.cloned.1.call-done = bf16[4,512,8192]{2,1,0:T(8,128)(2,1)} async-done(((bf16[4,128,8192]{2,1,0:T(8,128)(2,1)}), bf16[4,512,8192]{2,1,0:T(8,128)(2,1)}) %all-gather.24.cloned.1.call-update) | async-done | bytes 33554448 | tf_op jit(solution)/shard_map/all_gather | solution.py:21
  1097.3 17.8 all-gather.26.cloned.1.call-done
  1121.7 17.7 fusion.1
  1139.5 81.0 %all-gather.28.cloned.1.call-done = bf16[4,128,8192]{2,1,0:T(8,128)(2,1)} async-done(((bf16[4,32,8192]{2,1,0:T(8,128)(2,1)}), bf16[4,128,8192]{2,1,0:T(8,128)(2,1)}) %all-gather.28.cloned.1.call-update) | async-done | bytes 8388624 | tf_op jit(solution)/shard_map/all_gather | solution.py:20
  1220.6 294.1 %all-gather.30.cloned.1.call-done = bf16[4,512,8192]{2,1,0:T(8,128)(2,1)} async-done(((bf16[4,128,8192]{2,1,0:T(8,128)(2,1)}), bf16[4,512,8192]{2,1,0:T(8,128)(2,1)}) %all-gather.30.cloned.1.call-update) | async-done | bytes 33554448 | tf_op jit(solution)/shard_map/all_gather | solution.py:21
  1555.9 17.8 all-gather.32.cloned.1.call-done
  1579.8 17.7 fusion.2
  1597.7 81.0 %all-gather.34.cloned.1.call-done = bf16[4,128,8192]{2,1,0:T(8,128)(2,1)} async-done(((bf16[4,32,8192]{2,1,0:T(8,128)(2,1)}), bf16[4,128,8192]{2,1,0:T(8,128)(2,1)}) %all-gather.34.cloned.1.call-update) | async-done | bytes 8388624 | tf_op jit(solution)/shard_map/all_gather | solution.py:20
  1678.8 293.9 %all-gather.36.cloned.1.call-done = bf16[4,512,8192]{2,1,0:T(8,128)(2,1)} async-done(((bf16[4,128,8192]{2,1,0:T(8,128)(2,1)}), bf16[4,512,8192]{2,1,0:T(8,128)(2,1)}) %all-gather.36.cloned.1.call-update) | async-done | bytes 33554448 | tf_op jit(solution)/shard_map/all_gather | solution.py:21
  2013.9 17.8 all-gather.38.cloned.1.call-done
  2037.9 17.7 fusion.3
  2055.8 81.0 %all-gather.40.cloned.1.call-done = bf16[4,128,8192]{2,1,0:T(8,128)(2,1)} async-done(((bf16[4,32,8192]{2,1,0:T(8,128)(2,1)}), bf16[4,128,8192]{2,1,0:T(8,128)(2,1)}) %all-gather.40.cloned.1.call-update) | async-done | bytes 8388624 | tf_op jit(solution)/shard_map/all_gather | solution.py:20
  2136.9 294.1 %all-gather.42.cloned.1.call-done = bf16[4,512,8192]{2,1,0:T(8,128)(2,1)} async-done(((bf16[4,128,8192]{2,1,0:T(8,128)(2,1)}), bf16[4,512,8192]{2,1,0:T(8,128)(2,1)}) %all-gather.42.cloned.1.call-update) | async-done | bytes 33554448 | tf_op jit(solution)/shard_map/all_gather | solution.py:21
  2431.0 15.9 fusion.32
  2472.1 17.8 all-gather.44.cloned.1.call-done
  2496.1 19.7 fusion.7
  (89 shorter events, 229.7 us)
Async XLA Ops:
  7.2 160.8 %reduce-scatter.7.cloned.1.call-start = ((), (), s32[]{:S(2)}) async-start(), calls=%async_computation.6 | async-start | bytes 20971520 | tf_op jit(solution)/shard_map/reduce_scatter | solution.py:30
  18.6 284.9 %all-gather.16.cloned.1.call-start = ((), (), s32[]{:S(2)}) async-start(), calls=%async_computation.7 | async-start | bytes 10485760 | tf_op jit(solution)/shard_map/all_gather | solution.py:20
  224.8 373.0 %all-gather.18.cloned.1.call-start = ((), (), s32[]{:S(2)}) async-start(), calls=%async_computation.8 | async-start | bytes 41943040 | tf_op jit(solution)/shard_map/all_gather | solution.py:21
  303.6 294.2 %copy-start.4 = (bf16[4,32,8192]{2,1,0:T(8,128)(2,1)S(1)}, bf16[4,32,8192]{2,1,0:T(8,128)(2,1)}, u32[]{:S(2)}) copy-start(bf16[4,32,8192]{2,1,0:T(8,128)(2,1)} %divide_convert_fusion) | copy-start | bytes 6291460
  303.6 319.5 %reduce-scatter.9.cloned.1.call-start = ((), (), s32[]{:S(2)}) async-start(), calls=%async_computation.9 | async-start | bytes 393216 | tf_op jit(solution)/shard_map/reduce_scatter | solution.py:39
  613.7 43.1 %all-gather.20.cloned.1.call-start = ((), (), s32[]{:S(2)}) async-start(), calls=%async_computation.10 | async-start | bytes 1310720 | tf_op jit(solution)/shard_map/all_gather | solution.py:21
  634.8 127.1 %all-gather.22.cloned.1.call-start = ((), (), s32[]{:S(2)}) async-start(), calls=%async_computation.11 | async-start | bytes 10485760 | tf_op jit(solution)/shard_map/all_gather | solution.py:20
  680.9 375.2 %all-gather.24.cloned.1.call-start = ((), (), s32[]{:S(2)}) async-start(), calls=%async_computation.12 | async-start | bytes 41943040 | tf_op jit(solution)/shard_map/all_gather | solution.py:21
  761.9 294.2 %copy-start = (bf16[4,32,8192]{2,1,0:T(8,128)(2,1)S(1)}, bf16[4,32,8192]{2,1,0:T(8,128)(2,1)}, u32[]{:S(2)}) copy-start(bf16[4,32,8192]{2,1,0:T(8,128)(2,1)} %fusion) | copy-start | bytes 6291460
  762.0 319.5 %reduce-scatter.11.cloned.1.call-start = ((), (), s32[]{:S(2)}) async-start(), calls=%async_computation.13 | async-start | bytes 393216 | tf_op jit(solution)/shard_map/reduce_scatter | solution.py:39
  1072.0 43.1 %all-gather.26.cloned.1.call-start = ((), (), s32[]{:S(2)}) async-start(), calls=%async_computation.14 | async-start | bytes 1310720 | tf_op jit(solution)/shard_map/all_gather | solution.py:21
  1093.1 127.4 %all-gather.28.cloned.1.call-start = ((), (), s32[]{:S(2)}) async-start(), calls=%async_computation.15 | async-start | bytes 10485760 | tf_op jit(solution)/shard_map/all_gather | solution.py:20
  1139.4 375.3 %all-gather.30.cloned.1.call-start = ((), (), s32[]{:S(2)}) async-start(), calls=%async_computation.16 | async-start | bytes 41943040 | tf_op jit(solution)/shard_map/all_gather | solution.py:21
  1220.5 294.2 %copy-start.1 = (bf16[4,32,8192]{2,1,0:T(8,128)(2,1)S(1)}, bf16[4,32,8192]{2,1,0:T(8,128)(2,1)}, u32[]{:S(2)}) copy-start(bf16[4,32,8192]{2,1,0:T(8,128)(2,1)} %fusion.1) | copy-start | bytes 6291460
  1220.6 319.5 %reduce-scatter.13.cloned.1.call-start = ((), (), s32[]{:S(2)}) async-start(), calls=%async_computation.17 | async-start | bytes 393216 | tf_op jit(solution)/shard_map/reduce_scatter | solution.py:39
  1530.6 43.1 %all-gather.32.cloned.1.call-start = ((), (), s32[]{:S(2)}) async-start(), calls=%async_computation.18 | async-start | bytes 1310720 | tf_op jit(solution)/shard_map/all_gather | solution.py:21
  1551.7 127.0 %all-gather.34.cloned.1.call-start = ((), (), s32[]{:S(2)}) async-start(), calls=%async_computation.19 | async-start | bytes 10485760 | tf_op jit(solution)/shard_map/all_gather | solution.py:20
  1597.6 375.1 %all-gather.36.cloned.1.call-start = ((), (), s32[]{:S(2)}) async-start(), calls=%async_computation.20 | async-start | bytes 41943040 | tf_op jit(solution)/shard_map/all_gather | solution.py:21
  1678.8 319.3 %reduce-scatter.15.cloned.1.call-start = ((), (), s32[]{:S(2)}) async-start(), calls=%async_computation.21 | async-start | bytes 393216 | tf_op jit(solution)/shard_map/reduce_scatter | solution.py:39
  1988.7 43.1 %all-gather.38.cloned.1.call-start = ((), (), s32[]{:S(2)}) async-start(), calls=%async_computation.22 | async-start | bytes 1310720 | tf_op jit(solution)/shard_map/all_gather | solution.py:21
  2009.8 127.0 %all-gather.40.cloned.1.call-start = ((), (), s32[]{:S(2)}) async-start(), calls=%async_computation.23 | async-start | bytes 10485760 | tf_op jit(solution)/shard_map/all_gather | solution.py:20
  2055.7 375.2 %all-gather.42.cloned.1.call-start = ((), (), s32[]{:S(2)}) async-start(), calls=%async_computation.24 | async-start | bytes 41943040 | tf_op jit(solution)/shard_map/all_gather | solution.py:21
  2136.8 319.5 %reduce-scatter.17.cloned.1.call-start = ((), (), s32[]{:S(2)}) async-start(), calls=%async_computation.25 | async-start | bytes 393216 | tf_op jit(solution)/shard_map/reduce_scatter | solution.py:39
  2446.9 43.0 %all-gather.44.cloned.1.call-start = ((), (), s32[]{:S(2)}) async-start(), calls=%async_computation.26 | async-start | bytes 1310720 | tf_op jit(solution)/shard_map/all_gather | solution.py:21
  (2 other events, 588.2 us)
Sparse Core Ops, SparseCore 0:
  18.8 149.1 reduce-scatter.6
  224.9 78.6 all-gather.15
  305.2 292.5 all-gather.17
  613.8 9.2 reduce-scatter.8
  634.9 21.7 all-gather.19
  681.0 80.8 all-gather.21
  763.5 292.5 all-gather.23
  1072.1 9.2 reduce-scatter.10
  1093.2 21.8 all-gather.25
  1139.6 80.8 all-gather.27
  1222.1 292.5 all-gather.29
  1530.7 9.2 reduce-scatter.12
  1551.8 21.8 all-gather.31
  1597.8 80.8 all-gather.33
  1680.1 292.5 all-gather.35
  1988.8 9.2 reduce-scatter.14
  2009.9 21.8 all-gather.37
  2055.8 80.8 all-gather.39
  2138.3 292.5 all-gather.41
  2447.0 9.2 reduce-scatter.16
  2468.1 21.7 all-gather.43
where the time goes:
time: 2530 us; the launch traced here: 2520 us
  waiting for transfers between devices  2160 us (85%)
  matrix products  177 us (7%)
  blocking collectives  143 us (6%)
  other arithmetic  27.6 us (1%)
    all_gather x10, waiting for transfers between devices, gather_rows(): return lax.all_gather(x_mid, 'fsdp', axis=1, tiled=True)  1560 us
    all_gather x5, waiting for transfers between devices, gather_rows(): x_mid = lax.all_gather(x_blk, 'dp', axis=1, tiled=True)  403 us
    reduce_scatter x1, waiting for transfers between devices, local_step(): lax.psum_scatter(g_blk[0].astype(jnp.float32), 'dp', scatter_dimension=1,...  149 us
    dot_general x5, matrix products, local_step(): jnp.einsum('kij,kjn->kin', poly_rows, x_cols, preferred_element_type=jnp....  90.6 us
    dot_general x5, matrix products, local_step(): jnp.einsum('kin,kjn->kij', x_blk, x_cols, preferred_element_type=jnp.floa...  79.3 us
    all_gather x5, blocking collectives, gather_rows(): x_mid = lax.all_gather(x_blk, 'dp', axis=1, tiled=True)  53.4 us
  transfers between devices with their start and end apart: 21, of which 21 were waited for; matrix products, arithmetic and copies ran while one was open for 0% of the time, Pallas kernels for 0%

commit v1 on v0

v1 whole, which is shorter than its diff:
```python
import functools
import math
import jax
import jax.numpy as jnp
from jax import lax
from jax.experimental import pallas as pl
from jax.experimental.pallas import tpu as pltpu
from jax.sharding import PartitionSpec as P

MOMENTUM = 0.95
LEARN_RATE = 0.1
WEIGHT_DECAY = 0.1
COEF_A = 3.4445
COEF_B = -4.7750
COEF_C = 2.0315
NORM_EPS = 1e-7
NS_STEPS = 5
ROW_AXES = ('fsdp', 'dp')
F32 = jnp.float32
BF16 = jnp.bfloat16
MESH = pl.DeviceIdType.MESH
SIDE = 4
BLK = 128
TRI = ((0, 0), (0, 1), (1, 1), (0, 2), (0, 3), (1, 2), (1, 3), (2, 2), (2, 3), (3, 3))
SLOT = {ij: n for n, ij in enumerate(TRI)}
HALF = len(TRI) // 2


def muon_kernel(m_hbm, g_hbm, mnew_hbm, xfin_hbm,
                gown, grecv, relay, mbuf, x0, xrow, xfull, xfin,
                nown, npair, nall, part, drecv, red, rsrecv, agbuf, amat, bmat,
                load_sem, out_sem, gsend, grcv, nsend, nrcv, csend, crcv, bsend, brcv,
                dsend, drcv, rssend, rsrcv, agsend, agrcv, fwsend, fwrcv):
    n_mat, rows, cols = mbuf.shape
    quarter = cols // SIDE
    half = cols // 2
    y = lax.axis_index('dp')
    x = lax.axis_index('fsdp')
    t = lax.axis_index('tp')
    partner = {'tp': 1 - t}
    up = lax.rem(y + 1, SIDE)
    down = lax.rem(y + SIDE - 1, SIDE)
    far = lax.rem(y + 2, SIDE)

    def row_ds(i):
        return pl.ds(pl.multiple_of(i * rows, rows), rows)

    def quarter_ds(i):
        return pl.ds(pl.multiple_of(i * quarter, quarter), quarter)

    def mat_of(yy, xx):
        return (yy // 2) * 2 + xx // 2

    def pos_of(yy, xx):
        return (yy % 2) * 2 + xx % 2

    loads = []
    for k in range(n_mat):
        loads.append((pltpu.make_async_copy(g_hbm.at[k, row_ds(y), :], gown.at[k], load_sem.at[0, k]),
                      pltpu.make_async_copy(m_hbm.at[k], mbuf.at[k], load_sem.at[1, k])))
        for c in loads[-1]:
            c.start()

    others = [(oy, ox) for oy in range(SIDE) for ox in range(SIDE) if (oy, ox) != (0, 0)]

    def peer(off):
        return lax.rem(y + off[0], SIDE), lax.rem(x + off[1], SIDE)

    barrier = pltpu.get_barrier_semaphore()
    pl.semaphore_signal(barrier, inc=1, device_id=partner, device_id_type=MESH)
    for off in others:
        py, px = peer(off)
        pl.semaphore_signal(barrier, inc=1, device_id={'dp': py, 'fsdp': px}, device_id_type=MESH)
    pl.semaphore_wait(barrier, 1 + len(others))

    def remote(src, dst, ssem, rsem, dev):
        return pltpu.make_async_remote_copy(src_ref=src, dst_ref=dst, send_sem=ssem, recv_sem=rsem,
                                            device_id=dev, device_id_type=MESH)

    lo, hi = pl.ds(0, half), pl.ds(half, half)

    def grad_copies(k):
        to_up, to_down = {'dp': up}, {'dp': down}
        return (
            remote(g_hbm.at[k, row_ds(up), :], grecv.at[k, 0], gsend.at[k, 0], grcv.at[k, 0], to_up),
            remote(g_hbm.at[k, row_ds(down), :], grecv.at[k, 1], gsend.at[k, 1], grcv.at[k, 1], to_down),
            remote(g_hbm.at[k, row_ds(far), lo], relay.at[k, 0], gsend.at[k, 2], grcv.at[k, 2], to_up),
            remote(g_hbm.at[k, row_ds(far), hi], relay.at[k, 1], gsend.at[k, 3], grcv.at[k, 3], to_down),
            remote(relay.at[k, 0], grecv.at[k, 2, :, lo], gsend.at[k, 4], grcv.at[k, 4], to_up),
            remote(relay.at[k, 1], grecv.at[k, 2, :, hi], gsend.at[k, 5], grcv.at[k, 5], to_down),
        )

    gcopies = [grad_copies(k) for k in range(n_mat)]

    def issue_grad(k):
        for j in (2, 3, 0, 1):
            gcopies[k][j].start()

    issue_grad(0)
    issue_grad(1)
    step = min(512, cols)
    out_copies = []
    tile_rows = lax.broadcasted_iota(jnp.int32, (8, 128), 0)
    norm_tile = jnp.zeros((8, 128), F32)
    for k in range(n_mat):
        gcopies[k][2].wait_recv()
        gcopies[k][4].start()
        gcopies[k][3].wait_recv()
        gcopies[k][5].start()
        if k + 2 < n_mat:
            issue_grad(k + 2)
        for c in loads[k]:
            c.wait()
        for j in (0, 1, 4, 5):
            gcopies[k][j].wait_recv()

        def col_step(i, acc, k=k):
            cs = pl.ds(pl.multiple_of(i * step, step), step)
            g_sum = (gown[k, :, cs].astype(F32) + grecv[k, 0, :, cs].astype(F32)) + (
                grecv[k, 1, :, cs].astype(F32) + grecv[k, 2, :, cs].astype(F32))
            m_new = MOMENTUM * mbuf[k, :, cs] + g_sum
            mbuf[k, :, cs] = m_new
            x_zero = g_sum + MOMENTUM * m_new
            x0[k, :, cs] = x_zero
            return acc + x_zero * x_zero

        acc = lax.fori_loop(0, cols // step, col_step, jnp.zeros((rows, step), F32))
        norm_tile = jnp.where(tile_rows == k, jnp.sum(acc), norm_tile)
        oc = pltpu.make_async_copy(mbuf.at[k], mnew_hbm.at[k], out_sem.at[k])
        oc.start()
        out_copies.append(oc)

    nown[...] = norm_tile
    pair_copy = remote(nown, npair, nsend.at[0], nrcv.at[0], partner)
    pair_copy.start()
    pair_copy.wait_recv()
    here = y * SIDE + x
    nall[here] = nown[...] + npair[...]
    norm_copies = []
    for n, off in enumerate(others):
        py, px = peer(off)
        c = remote(nall.at[here], nall.at[here], nsend.at[1 + n], nrcv.at[1 + n], {'dp': py, 'fsdp': px})
        c.start()
        norm_copies.append(c)
    for c in norm_copies:
        c.wait_recv()
    sq_all = jnp.sum(nall[...], axis=0)
    denom_all = jnp.sqrt(sq_all) + NORM_EPS

    for k in range(n_mat):
        denom = denom_all[k:k + 1, 0:1]

        def div_step(i, carry, k=k, denom=denom):
            cs = pl.ds(pl.multiple_of(i * step, step), step)
            xrow[k, :, cs] = (x0[k, :, cs] / denom).astype(BF16)
            return carry

        lax.fori_loop(0, cols // step, div_step, 0)

    my_mat, my_pos, my_rows = mat_of(y, x), pos_of(y, x), x * SIDE + y
    col_copies = []
    for n, off in enumerate(others):
        py, px = peer(off)
        c = remote(xrow.at[mat_of(py, px), :, quarter_ds(pos_of(py, px))], xfull.at[row_ds(my_rows), :],
                   csend.at[n], crcv.at[n], {'dp': py, 'fsdp': px})
        c.start()
        col_copies.append(c)
    own = pltpu.make_async_copy(xrow.at[my_mat, :, quarter_ds(my_pos)], xfull.at[row_ds(my_rows), :], load_sem.at[0, 0])
    own.start()
    own.wait()
    for c in col_copies:
        c.wait_recv()

    fy, fx = y + 1 - 2 * (y % 2), x + 1 - 2 * (x % 2)
    square = ((y, fx), (fy, x), (fy, fx))
    chunk = HALF * BLK // 4

    def chunk_ds(pos):
        return pl.ds(pl.multiple_of(pos * chunk, chunk), chunk)

    def packed_ds(core, pos):
        return pl.ds(pl.multiple_of(core * (HALF * BLK) + pos * chunk, chunk), chunk)

    bcol = min(256, quarter)

    def pair_of(it):
        return remote(part.at[it, 1 - t], drecv.at[it], dsend.at[it], drcv.at[it], partner)

    def scatter_of(it, n):
        py, px = square[n]
        return remote(red.at[it, chunk_ds(pos_of(py, px)), :], rsrecv.at[it, n], rssend.at[it, n], rsrcv.at[it, n],
                      {'dp': py, 'fsdp': px})

    def gather_of(it, n):
        mine = agbuf.at[it, packed_ds(t, my_pos), :]
        py, px = square[n]
        return remote(mine, mine, agsend.at[it, n], agrcv.at[it, n], {'dp': py, 'fsdp': px})

    def forward_of(it, n):
        pos = my_pos if n == 0 else pos_of(*square[n - 1])
        held = agbuf.at[it, packed_ds(t, pos), :]
        return remote(held, held, fwsend.at[it, n], fwrcv.at[it, n], partner)

    def iteration(it, carry):
        for bi, bj in ((0, 0), (0, 1), (1, 1)):
            gram = lax.dot_general(xfull[2 * BLK * bi:2 * BLK * (bi + 1), :], xfull[2 * BLK * bj:2 * BLK * (bj + 1), :],
                                   (((1,), (1,)), ((), ())), preferred_element_type=F32)
            for a in range(2):
                for b in range(2):
                    n = SLOT.get((2 * bi + a, 2 * bj + b))
                    if n is not None:
                        part[it, n // HALF, (n % HALF) * BLK:(n % HALF + 1) * BLK, :] = (
                            gram[a * BLK:(a + 1) * BLK, b * BLK:(b + 1) * BLK])
        pair = pair_of(it)
        pair.start()
        pair.wait_recv()
        red[it] = part[it, t] + drecv[it]
        for n in range(3):
            scatter_of(it, n).start()
        for n in range(3):
            scatter_of(it, n).wait_recv()
        total = (red[it, chunk_ds(my_pos), :] + rsrecv[it, 0]) + (rsrecv[it, 1] + rsrecv[it, 2])
        agbuf[it, packed_ds(t, my_pos), :] = total.astype(BF16)
        for n in range(3):
            gather_of(it, n).start()
        forward_of(it, 0).start()
        for n in range(3):
            gather_of(it, n).wait_recv()
            forward_of(it, n + 1).start()
        for n in range(4):
            forward_of(it, n).wait_recv()
        for n, (bi, bj) in enumerate(TRI):
            block = agbuf[it, n * BLK:(n + 1) * BLK, :]
            amat[bi * BLK:(bi + 1) * BLK, bj * BLK:(bj + 1) * BLK] = block
            if bi != bj:
                amat[bj * BLK:(bj + 1) * BLK, bi * BLK:(bi + 1) * BLK] = block.astype(F32).T.astype(BF16)
        for bi in range(2):
            rs = slice(2 * BLK * bi, 2 * BLK * (bi + 1))
            sq = jnp.dot(amat[rs, :], amat[...], preferred_element_type=F32).astype(BF16)
            bmat[rs, :] = (COEF_B * amat[rs, :].astype(F32) + COEF_C * sq.astype(F32)).astype(BF16)

        def col_block(i, c2):
            cs = pl.ds(pl.multiple_of(i * bcol, bcol), bcol)
            x_old = xfull[:, cs]
            prod = jnp.dot(bmat[...], x_old, preferred_element_type=F32)
            xfull[:, cs] = (COEF_A * x_old.astype(F32) + prod).astype(BF16)
            return c2

        lax.fori_loop(0, quarter // bcol, col_block, 0)
        return carry

    for c in col_copies:
        c.wait_send()
    lax.fori_loop(0, NS_STEPS, iteration, 0)

    back_copies = []
    for n, off in enumerate(others):
        py, px = peer(off)
        c = remote(xfull.at[row_ds(px * SIDE + py), :], xfin.at[my_mat, :, quarter_ds(my_pos)],
                   bsend.at[n], brcv.at[n], {'dp': py, 'fsdp': px})
        c.start()
        back_copies.append(c)
    own = pltpu.make_async_copy(xfull.at[row_ds(my_rows), :], xfin.at[my_mat, :, quarter_ds(my_pos)], load_sem.at[0, 0])
    own.start()
    own.wait()
    for c in back_copies:
        c.wait_recv()
    fin = pltpu.make_async_copy(xfin, xfin_hbm, load_sem.at[0, 0])
    fin.start()

    for k in range(n_mat):
        for c in gcopies[k]:
            c.wait_send()
        out_copies[k].wait()
    pair_copy.wait_send()
    for c in norm_copies + back_copies:
        c.wait_send()

    def drain(it, carry):
        pair_of(it).wait_send()
        for n in range(3):
            scatter_of(it, n).wait_send()
            gather_of(it, n).wait_send()
        for n in range(4):
            forward_of(it, n).wait_send()
        return carry

    lax.fori_loop(0, NS_STEPS, drain, 0)
    fin.wait()


def run_kernel(m_blk, g_blk):
    n_mat, rows, cols = m_blk.shape
    all_rows = rows * SIDE * SIDE
    quarter = cols // SIDE
    packed = len(TRI) * BLK
    chunk = packed // 8
    n_oth = SIDE * SIDE - 1
    dma = pltpu.SemaphoreType.DMA
    scratch = [
        pltpu.VMEM((n_mat, rows, cols), BF16),
        pltpu.VMEM((n_mat, 3, rows, cols), BF16),
        pltpu.VMEM((n_mat, 2, rows, cols // 2), BF16),
        pltpu.VMEM((n_mat, rows, cols), F32),
        pltpu.VMEM((n_mat, rows, cols), F32),
        pltpu.VMEM((n_mat, rows, cols), BF16),
        pltpu.VMEM((all_rows, quarter), BF16),
        pltpu.VMEM((n_mat, rows, cols), BF16),
        pltpu.VMEM((8, 128), F32),
        pltpu.VMEM((8, 128), F32),
        pltpu.VMEM((SIDE * SIDE, 8, 128), F32),
        pltpu.VMEM((NS_STEPS, 2, packed // 2, BLK), F32),
        pltpu.VMEM((NS_STEPS, packed // 2, BLK), F32),
        pltpu.VMEM((NS_STEPS, packed // 2, BLK), F32),
        pltpu.VMEM((NS_STEPS, 3, chunk, BLK), F32),
        pltpu.VMEM((NS_STEPS, packed, BLK), BF16),
        pltpu.VMEM((all_rows, all_rows), BF16),
        pltpu.VMEM((all_rows, all_rows), BF16),
        dma((2, n_mat)), dma((n_mat,)), dma((n_mat, 6)), dma((n_mat, 6)),
        dma((n_oth + 1,)), dma((n_oth + 1,)), dma((n_oth,)), dma((n_oth,)), dma((n_oth,)), dma((n_oth,)),
        dma((NS_STEPS,)), dma((NS_STEPS,)), dma((NS_STEPS, 3)), dma((NS_STEPS, 3)),
        dma((NS_STEPS, 3)), dma((NS_STEPS, 3)), dma((NS_STEPS, 4)), dma((NS_STEPS, 4)),
    ]
    anyspace = pl.BlockSpec(memory_space=pl.ANY)
    return pl.pallas_call(
        muon_kernel,
        out_shape=(jax.ShapeDtypeStruct(m_blk.shape, F32), jax.ShapeDtypeStruct(m_blk.shape, BF16)),
        in_specs=[anyspace, anyspace],
        out_specs=(anyspace, anyspace),
        scratch_shapes=scratch,
        compiler_params=pltpu.CompilerParams(collective_id=0, has_side_effects=True, vmem_limit_bytes=60 * 2 ** 20),
        name='muon_group',
    )(m_blk, g_blk)


def solution(mesh):
    mat_spec = P('stage', ROW_AXES, 'tp')
    grad_spec = P(('stage', 'dp'), None, 'fsdp', 'tp')
    tp_size = mesh.shape['tp']

    def local_step(w_blk, m_blk, g_blk):
        m_new, x_fin = run_kernel(m_blk, g_blk.reshape(g_blk.shape[1:]))
        col_count = w_blk.shape[2] * tp_size
        update_scale = LEARN_RATE * 0.2 * math.sqrt(col_count)
        decay_factor = 1.0 - LEARN_RATE * WEIGHT_DECAY
        w_new = decay_factor * w_blk - update_scale * x_fin.astype(F32)
        return w_new, m_new

    return jax.shard_map(local_step, mesh=mesh, in_specs=(mat_spec, mat_spec, grad_spec), out_specs=(mat_spec, mat_spec), check_vma=False)
```

time: 2530 us -> 273 us (0.11)
  waiting for transfers between devices: 2160 us -> 0 us
  Pallas kernels: 0 us -> 264 us
  matrix products: 177 us -> 0 us
  blocking collectives: 143 us -> 0 us
    all_gather x15 -> x0, waiting for transfers between devices: 1960 us -> none  [the longest x10 1560 us: gather_rows(): return lax.all_gather(x_mid, 'fsdp', axis=1, tiled=True)]
    pallas_call x0 -> x1, Pallas kernels: none -> 264 us  [run_kernel(): pl.pallas_call(muon_kernel, out_shape=(jax.ShapeDtypeStruct(m_blk.shape,...]
    reduce_scatter x6 -> x0, waiting for transfers between devices: 196 us -> none  [the longest x1 149 us: local_step(): lax.psum_scatter(g_blk[0].astype(jnp.float32), 'dp', scatter_dimension=1,...]
    dot_general x15 -> x0, matrix products: 177 us -> none  [the longest x5 90.6 us: local_step(): jnp.einsum('kij,kjn->kin', poly_rows, x_cols, preferred_element_type=jnp....]
    all_gather x15 -> x0, blocking collectives: 97.5 us -> none  [the longest x5 53.4 us: gather_rows(): x_mid = lax.all_gather(x_blk, 'dp', axis=1, tiled=True)]
    psum x1 -> x0, blocking collectives: 45.1 us -> none  [local_step(): sq_sum = lax.psum(jnp.sum(x_zero * x_zero, axis=(1, 2)), GROUP_AXES)]
  transfers between devices with their start and end apart: 21 -> 0, of which waited for: 21 -> 0; matrix products, arithmetic and copies ran while one was open for 0% -> 0% of each run, Pallas kernels for 0% -> 0%
where the time goes in v1:
time: 273 us; the launch traced here: 272 us
  Pallas kernels  264 us (97%)
  other arithmetic  5.64 us (2%)
    pallas_call x1, Pallas kernels, run_kernel(): pl.pallas_call(muon_kernel, out_shape=(jax.ShapeDtypeStruct(m_blk.shape,...  264 us
    sub x1, other arithmetic, local_step(): w_new = decay_factor * w_blk - update_scale * x_fin.astype(F32)  5.64 us

profile of v1, /device:TPU:97, one launch (start us, length us, event | category | flops | bytes accessed | tf_op | source)
XLA Modules:
  0.0 272.4 jit_solution(5652618479788378670)
XLA Ops:
  0.6 264.1 %muon_group.1 = (f32[4,32,8192]{2,1,0:T(8,128)}, bf16[4,32,8192]{2,1,0:T(8,128)(2,1)}) custom-call(f32[4,32,8192]{2,1,0:T(8,128)} %m_hbm.1, bf16[4,128,8192]{2,1,0:T(8,128)(2,1)} %bitcast.1), custom_call_target="tpu_custom_call" | custom-call | tf_op jit(solution)/shard_map/muon_group/pallas_call | solution.py:325
  264.8 0.0 copy-start
  264.8 5.6 %multiply_subtract_fusion = f32[4,32,8192]{2,1,0:T(8,128)} fusion(bf16[4,32,8192]{2,1,0:T(8,128)(2,1)} %get-tuple-element.4, f32[4,32,8192]{2,1,0:T(8,128)} %param.3), kind=kLoop, calls=%fused_computation | loop fusion | flops 4194304 | bytes 10485760 | tf_op jit(solution)/shard_map/sub | solution.py:346
  270.4 0.0 copy-done
  270.4 2.0 copy.6
Async XLA Ops:
  264.8 5.6 %copy-start = (f32[4,32,8192]{2,1,0:T(8,128)S(1)}, f32[4,32,8192]{2,1,0:T(8,128)}, u32[]{:S(2)}) copy-start(f32[4,32,8192]{2,1,0:T(8,128)} %get-tuple-element.9) | copy-start | bytes 12582916

commit v2 on v1

--- a/solution.py
+++ b/solution.py
@@ -19,18 +19,20 @@
 F32 = jnp.float32
 BF16 = jnp.bfloat16
 MESH = pl.DeviceIdType.MESH
+VMEM_MIB = 44
 SIDE = 4
 BLK = 128
 TRI = ((0, 0), (0, 1), (1, 1), (0, 2), (0, 3), (1, 2), (1, 3), (2, 2), (2, 3), (3, 3))
 SLOT = {ij: n for n, ij in enumerate(TRI)}
 HALF = len(TRI) // 2
+RELAYED = (((0, 3), (0, 2)), ((0, 3), (1, 2)), ((3, 0), (2, 0)), ((3, 0), (2, 1)))
 
 
 def muon_kernel(m_hbm, g_hbm, mnew_hbm, xfin_hbm,
                 gown, grecv, relay, mbuf, x0, xrow, xfull, xfin,
-                nown, npair, nall, part, drecv, red, rsrecv, agbuf, amat, bmat,
+                nown, npair, nall, part, drecv, red, rsrecv, agbuf, amat, bmat, cheld, bheld,
                 load_sem, out_sem, gsend, grcv, nsend, nrcv, csend, crcv, bsend, brcv,
-                dsend, drcv, rssend, rsrcv, agsend, agrcv, fwsend, fwrcv):
+                dsend, drcv, rssend, rsrcv, agsend, agrcv, fwsend, fwrcv, chsem, bhsem):
     n_mat, rows, cols = mbuf.shape
     quarter = cols // SIDE
     half = cols // 2
@@ -157,19 +159,39 @@
 
         lax.fori_loop(0, cols // step, div_step, 0)
 
+    def exchange(src_of, dst_of, held, ssem, rsem, hsem):
+        def to(off):
+            py, px = peer(off)
+            return {'dp': py, 'fsdp': px}
+
+        def origin(off):
+            return lax.rem(y + SIDE - off[0], SIDE), lax.rem(x + SIDE - off[1], SIDE)
+
+        first, second, direct = [], [], []
+        for n, (station, off) in enumerate(RELAYED):
+            i = others.index(off)
+            first.append(remote(src_of(*peer(off)), held.at[n], hsem.at[0, n], hsem.at[1, n], to(station)))
+            hop = ((off[0] - station[0]) % SIDE, (off[1] - station[1]) % SIDE)
+            second.append(remote(held.at[n], dst_of(*origin(station)), ssem.at[i], rsem.at[i], to(hop)))
+        relayed = [off for _, off in RELAYED]
+        for i, off in enumerate(others):
+            if off not in relayed:
+                direct.append(remote(src_of(*peer(off)), dst_of(y, x), ssem.at[i], rsem.at[i], to(off)))
+        for c in first + direct:
+            c.start()
+        own = pltpu.make_async_copy(src_of(y, x), dst_of(y, x), load_sem.at[0, 0])
+        own.start()
+        for c, f in zip(first, second):
+            c.wait_recv()
+            f.start()
+        own.wait()
+        for c in direct + second:
+            c.wait_recv()
+        return first + second + direct
+
     my_mat, my_pos, my_rows = mat_of(y, x), pos_of(y, x), x * SIDE + y
-    col_copies = []
-    for n, off in enumerate(others):
-        py, px = peer(off)
-        c = remote(xrow.at[mat_of(py, px), :, quarter_ds(pos_of(py, px))], xfull.at[row_ds(my_rows), :],
-                   csend.at[n], crcv.at[n], {'dp': py, 'fsdp': px})
-        c.start()
-        col_copies.append(c)
-    own = pltpu.make_async_copy(xrow.at[my_mat, :, quarter_ds(my_pos)], xfull.at[row_ds(my_rows), :], load_sem.at[0, 0])
-    own.start()
-    own.wait()
-    for c in col_copies:
-        c.wait_recv()
+    col_copies = exchange(lambda py, px: xrow.at[mat_of(py, px), :, quarter_ds(pos_of(py, px))],
+                          lambda oy, ox: xfull.at[row_ds(ox * SIDE + oy), :], cheld, csend, crcv, chsem)
 
     fy, fx = y + 1 - 2 * (y % 2), x + 1 - 2 * (x % 2)
     square = ((y, fx), (fy, x), (fy, fx))
@@ -239,32 +261,19 @@
             sq = jnp.dot(amat[rs, :], amat[...], preferred_element_type=F32).astype(BF16)
             bmat[rs, :] = (COEF_B * amat[rs, :].astype(F32) + COEF_C * sq.astype(F32)).astype(BF16)
 
-        def col_block(i, c2):
-            cs = pl.ds(pl.multiple_of(i * bcol, bcol), bcol)
+        for i in range(quarter // bcol):
+            cs = slice(i * bcol, (i + 1) * bcol)
             x_old = xfull[:, cs]
             prod = jnp.dot(bmat[...], x_old, preferred_element_type=F32)
             xfull[:, cs] = (COEF_A * x_old.astype(F32) + prod).astype(BF16)
-            return c2
-
-        lax.fori_loop(0, quarter // bcol, col_block, 0)
         return carry
 
     for c in col_copies:
         c.wait_send()
     lax.fori_loop(0, NS_STEPS, iteration, 0)
 
-    back_copies = []
-    for n, off in enumerate(others):
-        py, px = peer(off)
-        c = remote(xfull.at[row_ds(px * SIDE + py), :], xfin.at[my_mat, :, quarter_ds(my_pos)],
-                   bsend.at[n], brcv.at[n], {'dp': py, 'fsdp': px})
-        c.start()
-        back_copies.append(c)
-    own = pltpu.make_async_copy(xfull.at[row_ds(my_rows), :], xfin.at[my_mat, :, quarter_ds(my_pos)], load_sem.at[0, 0])
-    own.start()
-    own.wait()
-    for c in back_copies:
-        c.wait_recv()
+    back_copies = exchange(lambda py, px: xfull.at[row_ds(px * SIDE + py), :],
+                           lambda oy, ox: xfin.at[mat_of(oy, ox), :, quarter_ds(pos_of(oy, ox))], bheld, bsend, brcv, bhsem)
     fin = pltpu.make_async_copy(xfin, xfin_hbm, load_sem.at[0, 0])
     fin.start()
 
@@ -316,10 +325,13 @@
         pltpu.VMEM((NS_STEPS, packed, BLK), BF16),
         pltpu.VMEM((all_rows, all_rows), BF16),
         pltpu.VMEM((all_rows, all_rows), BF16),
+        pltpu.VMEM((len(RELAYED), rows, quarter), BF16),
+        pltpu.VMEM((len(RELAYED), rows, quarter), BF16),
         dma((2, n_mat)), dma((n_mat,)), dma((n_mat, 6)), dma((n_mat, 6)),
         dma((n_oth + 1,)), dma((n_oth + 1,)), dma((n_oth,)), dma((n_oth,)), dma((n_oth,)), dma((n_oth,)),
         dma((NS_STEPS,)), dma((NS_STEPS,)), dma((NS_STEPS, 3)), dma((NS_STEPS, 3)),
         dma((NS_STEPS, 3)), dma((NS_STEPS, 3)), dma((NS_STEPS, 4)), dma((NS_STEPS, 4)),
+        dma((2, len(RELAYED))), dma((2, len(RELAYED))),
     ]
     anyspace = pl.BlockSpec(memory_space=pl.ANY)
     return pl.pallas_call(
@@ -328,7 +340,7 @@
         in_specs=[anyspace, anyspace],
         out_specs=(anyspace, anyspace),
         scratch_shapes=scratch,
-        compiler_params=pltpu.CompilerParams(collective_id=0, has_side_effects=True, vmem_limit_bytes=60 * 2 ** 20),
+        compiler_params=pltpu.CompilerParams(collective_id=0, has_side_effects=True, vmem_limit_bytes=VMEM_MIB * 2 ** 20),
         name='muon_group',
     )(m_blk, g_blk)
 

time: 273 us -> 264 us (0.967)
  Pallas kernels: 264 us -> 258 us
  other arithmetic: 5.64 us -> 2.67 us
    pallas_call x1, Pallas kernels: 264 us -> 258 us  [run_kernel(): pl.pallas_call(muon_kernel, out_shape=(jax.ShapeDtypeStruct(m_blk.shape,...]
    sub x1, other arithmetic: 5.64 us -> 2.67 us  [local_step(): w_new = decay_factor * w_blk - update_scale * x_fin.astype(F32)]
where the time goes in v2:
time: 264 us
  Pallas kernels  258 us (98%)
  other arithmetic  2.67 us (1%)
    pallas_call x1, Pallas kernels, run_kernel(): pl.pallas_call(muon_kernel, out_shape=(jax.ShapeDtypeStruct(m_blk.shape,...  258 us

profile of v2, /device:TPU:97, one launch (start us, length us, event | category | flops | bytes accessed | tf_op | source)
XLA Modules:
  0.0 263.5 jit_solution(9173874035303598368)
XLA Ops:
  0.6 0.0 copy-start
  0.6 258.2 %muon_group.1 = (f32[4,32,8192]{2,1,0:T(8,128)S(1)}, bf16[4,32,8192]{2,1,0:T(8,128)(2,1)S(1)}) custom-call(f32[4,32,8192]{2,1,0:T(8,128)} %m_hbm.1, bf16[4,128,8192]{2,1,0:T(8,128)(2,1)} %bitcast.1), custom_call_target="tpu_custom_call" | custom-call | tf_op jit(solution)/shard_map/muon_group/pallas_call | solution.py:337
  258.8 0.0 copy-done
  258.8 2.7 %multiply_subtract_fusion = f32[4,32,8192]{2,1,0:T(8,128)} fusion(bf16[4,32,8192]{2,1,0:T(8,128)(2,1)S(1)} %get-tuple-element.4, f32[4,32,8192]{2,1,0:T(8,128)S(1)} %copy-done), kind=kLoop, calls=%fused_computation | loop fusion | flops 4194304 | bytes 10485760 | tf_op jit(solution)/shard_map/sub | solution.py:358
  261.5 2.0 copy.6
Async XLA Ops:
  0.6 258.2 %copy-start = (f32[4,32,8192]{2,1,0:T(8,128)S(1)}, f32[4,32,8192]{2,1,0:T(8,128)}, u32[]{:S(2)}) copy-start(f32[4,32,8192]{2,1,0:T(8,128)} %param.3) | copy-start | bytes 12582916

commit v3 on v1

--- a/solution.py
+++ b/solution.py
@@ -19,17 +19,19 @@
 F32 = jnp.float32
 BF16 = jnp.bfloat16
 MESH = pl.DeviceIdType.MESH
+VMEM_MIB = 47
 SIDE = 4
 BLK = 128
-TRI = ((0, 0), (0, 1), (1, 1), (0, 2), (0, 3), (1, 2), (1, 3), (2, 2), (2, 3), (3, 3))
-SLOT = {ij: n for n, ij in enumerate(TRI)}
+TRI = ((0, 0), (0, 1), (1, 1), (0, 2), (0, 3), (2, 2), (2, 3), (3, 3), (1, 2), (1, 3))
 HALF = len(TRI) // 2
 
 
 def muon_kernel(m_hbm, g_hbm, mnew_hbm, xfin_hbm,
                 gown, grecv, relay, mbuf, x0, xrow, xfull, xfin,
                 nown, npair, nall, part, drecv, red, rsrecv, agbuf, amat, bmat,
-                load_sem, out_sem, gsend, grcv, nsend, nrcv, csend, crcv, bsend, brcv,
+                cmid, chold1, chold2, bmid, bhold1, bhold2,
+                load_sem, out_sem, gsend, grcv, nsend, nrcv, csend, cmsem, ch1sem, ch2sem, cfsem,
+                bsend, bmsem, bh1sem, bh2sem, bfsem,
                 dsend, drcv, rssend, rsrcv, agsend, agrcv, fwsend, fwrcv):
     n_mat, rows, cols = mbuf.shape
     quarter = cols // SIDE
@@ -157,19 +159,97 @@
 
         lax.fori_loop(0, cols // step, div_step, 0)
 
-    my_mat, my_pos, my_rows = mat_of(y, x), pos_of(y, x), x * SIDE + y
-    col_copies = []
-    for n, off in enumerate(others):
-        py, px = peer(off)
-        c = remote(xrow.at[mat_of(py, px), :, quarter_ds(pos_of(py, px))], xfull.at[row_ds(my_rows), :],
-                   csend.at[n], crcv.at[n], {'dp': py, 'fsdp': px})
-        c.start()
-        col_copies.append(c)
-    own = pltpu.make_async_copy(xrow.at[my_mat, :, quarter_ds(my_pos)], xfull.at[row_ds(my_rows), :], load_sem.at[0, 0])
-    own.start()
-    own.wait()
-    for c in col_copies:
-        c.wait_recv()
+    def exchange(src_of, dst_of, dst_all, mid, hold1, hold2, ssem, msem, h1sem, h2sem, fsem):
+        sends = []
+
+        def send(src, dst, rsem, dev):
+            c = remote(src, dst, ssem.at[len(sends)], rsem, dev)
+            c.start()
+            sends.append(c)
+
+        locals_ = []
+        ways = []
+        for h in range(2):
+            p, q = (x, y) if h == 0 else (y, x)
+            near = [(lax.rem(c + 1, SIDE), lax.rem(c + SIDE - 1, SIDE), lax.rem(c + 2, SIDE)) for c in (p, q)]
+
+            def yx(pp, qq, h=h):
+                return (qq, pp) if h == 0 else (pp, qq)
+
+            def dev(pp, qq, yx=yx):
+                return dict(zip(('dp', 'fsdp'), yx(pp, qq)))
+
+            def src(pp, qq, h=h, yx=yx):
+                return src_of(*yx(pp, qq), h)
+
+            def dst(pp, qq, h=h, yx=yx):
+                return dst_of(*yx(pp, qq), h)
+
+            ways.append((p, q, near[0], near[1], dev, src, dst))
+
+        def second(h, o, piece):
+            p, q, (pu, pd, pf), (qu, qd, qf), dev, src, dst = ways[h]
+            start_p = (pd, pu, pf, p)[o]
+            send(piece(qu), dst(start_p, q), fsem, dev(p, qu))
+            send(piece(qd), dst(start_p, q), fsem, dev(p, qd))
+            side, i = ((0, 1), (1, 0), (1, 1), (0, 0))[o]
+            send(piece(qf), hold2.at[h, side, i], h2sem.at[h, side, i], dev(p, (qu, qd)[side]))
+            c = pltpu.make_async_copy(piece(q), dst(start_p, q), fsem)
+            c.start()
+
+        def relay2(h, o):
+            p, q, (pu, pd, pf), (qu, qd, qf), dev, src, dst = ways[h]
+            start_p = (pd, pu, pf, p)[o]
+            side, i = ((0, 1), (1, 0), (1, 1), (0, 0))[o]
+            held = hold2.at[h, side, i]
+            pltpu.make_async_copy(held, held, h2sem.at[h, side, i]).wait()
+            send(held, dst(start_p, (qd, qu)[side]), fsem, dev(p, (qu, qd)[side]))
+
+        for h in range(2):
+            p, q, (pu, pd, pf), _, dev, src, dst = ways[h]
+            for side, to in ((0, pu), (1, pd)):
+                for i in range(2):
+                    send(src(pf, 2 * side + i), hold1.at[h, side, i], h1sem.at[h, side], dev(to, q))
+        for i in range(SIDE):
+            for h in range(2):
+                p, q, (pu, pd, pf), _, dev, src, dst = ways[h]
+                for side, to in ((0, pu), (1, pd)):
+                    send(src(to, i), mid.at[h, side, i], msem.at[h, side], dev(to, q))
+        for h in range(2):
+            second(h, 3, lambda qq, h=h: ways[h][5](ways[h][0], qq))
+        for h in range(2):
+            p, q, (pu, pd, pf), _, dev, src, dst = ways[h]
+            for side, to in ((0, pu), (1, pd)):
+                held = hold1.at[h, side]
+                pltpu.make_async_copy(held, held, h1sem.at[h, side]).wait()
+                send(held, mid.at[h, 2, 2 * side:2 * side + 2], msem.at[h, 2 + side], dev(to, q))
+        for side in range(2):
+            for h in range(2):
+                got = mid.at[h, side]
+                pltpu.make_async_copy(got, got, msem.at[h, side]).wait()
+                second(h, side, lambda qq, h=h, side=side: mid.at[h, side, qq])
+        for h in range(2):
+            relay2(h, 3)
+        for h in range(2):
+            for side in range(2):
+                got = mid.at[h, 2, 2 * side:2 * side + 2]
+                pltpu.make_async_copy(got, got, msem.at[h, 2 + side]).wait()
+            second(h, 2, lambda qq, h=h: mid.at[h, 2, qq])
+        for o in (0, 1, 2):
+            for h in range(2):
+                relay2(h, o)
+        pltpu.make_async_copy(dst_all, dst_all, fsem).wait()
+        return sends
+
+    half_piece = quarter // 2
+
+    def piece_ds(pos, h):
+        return pl.ds(pl.multiple_of(pos * quarter + h * half_piece, half_piece), half_piece)
+
+    my_mat, my_pos = mat_of(y, x), pos_of(y, x)
+    col_copies = exchange(lambda py, px, h: xrow.at[mat_of(py, px), :, piece_ds(pos_of(py, px), h)],
+                          lambda oy, ox, h: xfull.at[row_ds(ox * SIDE + oy), h * half_piece:(h + 1) * half_piece],
+                          xfull, cmid, chold1, chold2, csend, cmsem, ch1sem, ch2sem, cfsem)
 
     fy, fx = y + 1 - 2 * (y % 2), x + 1 - 2 * (x % 2)
     square = ((y, fx), (fy, x), (fy, fx))
@@ -201,18 +281,22 @@
         held = agbuf.at[it, packed_ds(t, pos), :]
         return remote(held, held, fwsend.at[it, n], fwrcv.at[it, n], partner)
 
+    def half_gram(it, h):
+        nt = (((1,), (1,)), ((), ()))
+        pair_rows = xfull[pl.ds(pl.multiple_of(h * 2 * BLK, 2 * BLK), 2 * BLK), :]
+        square_gram = lax.dot_general(pair_rows, pair_rows, nt, preferred_element_type=F32)
+        cross_gram = lax.dot_general(xfull[pl.ds(pl.multiple_of(h * BLK, BLK), BLK), :], xfull[2 * BLK:, :], nt,
+                                     preferred_element_type=F32)
+        blocks = (square_gram[:BLK, :BLK], square_gram[:BLK, BLK:], square_gram[BLK:, BLK:],
+                  cross_gram[:, :BLK], cross_gram[:, BLK:])
+        for n, block in enumerate(blocks):
+            part[it, h, n * BLK:(n + 1) * BLK, :] = block
+
     def iteration(it, carry):
-        for bi, bj in ((0, 0), (0, 1), (1, 1)):
-            gram = lax.dot_general(xfull[2 * BLK * bi:2 * BLK * (bi + 1), :], xfull[2 * BLK * bj:2 * BLK * (bj + 1), :],
-                                   (((1,), (1,)), ((), ())), preferred_element_type=F32)
-            for a in range(2):
-                for b in range(2):
-                    n = SLOT.get((2 * bi + a, 2 * bj + b))
-                    if n is not None:
-                        part[it, n // HALF, (n % HALF) * BLK:(n % HALF + 1) * BLK, :] = (
-                            gram[a * BLK:(a + 1) * BLK, b * BLK:(b + 1) * BLK])
+        half_gram(it, 1 - t)
         pair = pair_of(it)
         pair.start()
+        half_gram(it, t)
         pair.wait_recv()
         red[it] = part[it, t] + drecv[it]
         for n in range(3):
@@ -239,32 +323,20 @@
             sq = jnp.dot(amat[rs, :], amat[...], preferred_element_type=F32).astype(BF16)
             bmat[rs, :] = (COEF_B * amat[rs, :].astype(F32) + COEF_C * sq.astype(F32)).astype(BF16)
 
-        def col_block(i, c2):
-            cs = pl.ds(pl.multiple_of(i * bcol, bcol), bcol)
+        for i in range(quarter // bcol):
+            cs = slice(i * bcol, (i + 1) * bcol)
             x_old = xfull[:, cs]
             prod = jnp.dot(bmat[...], x_old, preferred_element_type=F32)
             xfull[:, cs] = (COEF_A * x_old.astype(F32) + prod).astype(BF16)
-            return c2
-
-        lax.fori_loop(0, quarter // bcol, col_block, 0)
         return carry
 
     for c in col_copies:
         c.wait_send()
     lax.fori_loop(0, NS_STEPS, iteration, 0)
 
-    back_copies = []
-    for n, off in enumerate(others):
-        py, px = peer(off)
-        c = remote(xfull.at[row_ds(px * SIDE + py), :], xfin.at[my_mat, :, quarter_ds(my_pos)],
-                   bsend.at[n], brcv.at[n], {'dp': py, 'fsdp': px})
-        c.start()
-        back_copies.append(c)
-    own = pltpu.make_async_copy(xfull.at[row_ds(my_rows), :], xfin.at[my_mat, :, quarter_ds(my_pos)], load_sem.at[0, 0])
-    own.start()
-    own.wait()
-    for c in back_copies:
-        c.wait_recv()
+    back_copies = exchange(lambda py, px, h: xfull.at[row_ds(px * SIDE + py), h * half_piece:(h + 1) * half_piece],
+                           lambda oy, ox, h: xfin.at[mat_of(oy, ox), :, piece_ds(pos_of(oy, ox), h)],
+                           xfin, bmid, bhold1, bhold2, bsend, bmsem, bh1sem, bh2sem, bfsem)
     fin = pltpu.make_async_copy(xfin, xfin_hbm, load_sem.at[0, 0])
     fin.start()
 
@@ -297,6 +369,13 @@
     chunk = packed // 8
     n_oth = SIDE * SIDE - 1
     dma = pltpu.SemaphoreType.DMA
+    half_piece = (rows, quarter // 2)
+    relays = [
+        pltpu.VMEM((2, 3, SIDE) + half_piece, BF16),
+        pltpu.VMEM((2, 2, 2) + half_piece, BF16),
+        pltpu.VMEM((2, 2, 2) + half_piece, BF16),
+    ]
+    relay_sems = [dma((60,)), dma((2, 4)), dma((2, 2)), dma((2, 2, 2)), dma]
     scratch = [
         pltpu.VMEM((n_mat, rows, cols), BF16),
         pltpu.VMEM((n_mat, 3, rows, cols), BF16),
@@ -316,8 +395,9 @@
         pltpu.VMEM((NS_STEPS, packed, BLK), BF16),
         pltpu.VMEM((all_rows, all_rows), BF16),
         pltpu.VMEM((all_rows, all_rows), BF16),
+        *relays, *relays,
         dma((2, n_mat)), dma((n_mat,)), dma((n_mat, 6)), dma((n_mat, 6)),
-        dma((n_oth + 1,)), dma((n_oth + 1,)), dma((n_oth,)), dma((n_oth,)), dma((n_oth,)), dma((n_oth,)),
+        dma((n_oth + 1,)), dma((n_oth + 1,)), *relay_sems, *relay_sems,
         dma((NS_STEPS,)), dma((NS_STEPS,)), dma((NS_STEPS, 3)), dma((NS_STEPS, 3)),
         dma((NS_STEPS, 3)), dma((NS_STEPS, 3)), dma((NS_STEPS, 4)), dma((NS_STEPS, 4)),
     ]
@@ -328,7 +408,7 @@
         in_specs=[anyspace, anyspace],
         out_specs=(anyspace, anyspace),
         scratch_shapes=scratch,
-        compiler_params=pltpu.CompilerParams(collective_id=0, has_side_effects=True, vmem_limit_bytes=60 * 2 ** 20),
+        compiler_params=pltpu.CompilerParams(collective_id=0, has_side_effects=True, vmem_limit_bytes=VMEM_MIB * 2 ** 20),
         name='muon_group',
     )(m_blk, g_blk)
 

time: 273 us -> 243 us (0.89)
  Pallas kernels: 264 us -> 237 us
  other arithmetic: 5.64 us -> 2.67 us
    pallas_call x1, Pallas kernels: 264 us -> 237 us  [run_kernel(): pl.pallas_call(muon_kernel, out_shape=(jax.ShapeDtypeStruct(m_blk.shape,...]
    sub x1, other arithmetic: 5.64 us -> 2.67 us  [local_step(): w_new = decay_factor * w_blk - update_scale * x_fin.astype(F32)]
where the time goes in v3:
time: 243 us; the launch traced here: 242 us
  Pallas kernels  237 us (98%)
  other arithmetic  2.67 us (1%)
    pallas_call x1, Pallas kernels, run_kernel(): pl.pallas_call(muon_kernel, out_shape=(jax.ShapeDtypeStruct(m_blk.shape,...  237 us

profile of v3, /device:TPU:97, one launch (start us, length us, event | category | flops | bytes accessed | tf_op | source)
XLA Modules:
  0.0 242.4 jit_solution(13599564272590422096)
XLA Ops:
  0.6 0.0 copy-start
  0.6 237.1 %muon_group.1 = (f32[4,32,8192]{2,1,0:T(8,128)S(1)}, bf16[4,32,8192]{2,1,0:T(8,128)(2,1)S(1)}) custom-call(f32[4,32,8192]{2,1,0:T(8,128)} %m_hbm.1, bf16[4,128,8192]{2,1,0:T(8,128)(2,1)} %bitcast.1), custom_call_target="tpu_custom_call" | custom-call | tf_op jit(solution)/shard_map/muon_group/pallas_call | solution.py:405
  237.8 0.0 copy-done
  237.8 2.7 %multiply_subtract_fusion = f32[4,32,8192]{2,1,0:T(8,128)} fusion(bf16[4,32,8192]{2,1,0:T(8,128)(2,1)S(1)} %get-tuple-element.4, f32[4,32,8192]{2,1,0:T(8,128)S(1)} %copy-done), kind=kLoop, calls=%fused_computation | loop fusion | flops 4194304 | bytes 10485760 | tf_op jit(solution)/shard_map/sub | solution.py:426
  240.4 2.0 copy.6
Async XLA Ops:
  0.6 237.1 %copy-start = (f32[4,32,8192]{2,1,0:T(8,128)S(1)}, f32[4,32,8192]{2,1,0:T(8,128)}, u32[]{:S(2)}) copy-start(f32[4,32,8192]{2,1,0:T(8,128)} %param.3) | copy-start | bytes 12582916

commit v4 on v3

--- a/solution.py
+++ b/solution.py
@@ -24,15 +24,16 @@
 BLK = 128
 TRI = ((0, 0), (0, 1), (1, 1), (0, 2), (0, 3), (2, 2), (2, 3), (3, 3), (1, 2), (1, 3))
 HALF = len(TRI) // 2
+PLACE = ((0, 1), (1, 0), (1, 1), (0, 0))
 
 
 def muon_kernel(m_hbm, g_hbm, mnew_hbm, xfin_hbm,
-                gown, grecv, relay, mbuf, x0, xrow, xfull, xfin,
+                gown, grecv, relay, mbuf, x0, xrow, xfull,
                 nown, npair, nall, part, drecv, red, rsrecv, agbuf, amat, bmat,
                 cmid, chold1, chold2, bmid, bhold1, bhold2,
                 load_sem, out_sem, gsend, grcv, nsend, nrcv, csend, cmsem, ch1sem, ch2sem, cfsem,
                 bsend, bmsem, bh1sem, bh2sem, bfsem,
-                dsend, drcv, rssend, rsrcv, agsend, agrcv, fwsend, fwrcv):
+                dsend, drcv, rssend, rsrcv, agsend, agrcv, fwsend, fwrcv, round_sem):
     n_mat, rows, cols = mbuf.shape
     quarter = cols // SIDE
     half = cols // 2
@@ -68,12 +69,12 @@
     def peer(off):
         return lax.rem(y + off[0], SIDE), lax.rem(x + off[1], SIDE)
 
+    xup, xdown = lax.rem(x + 1, SIDE), lax.rem(x + SIDE - 1, SIDE)
+    neighbours = ({'dp': up}, {'dp': down}, {'fsdp': xup}, {'fsdp': xdown})
     barrier = pltpu.get_barrier_semaphore()
-    pl.semaphore_signal(barrier, inc=1, device_id=partner, device_id_type=MESH)
-    for off in others:
-        py, px = peer(off)
-        pl.semaphore_signal(barrier, inc=1, device_id={'dp': py, 'fsdp': px}, device_id_type=MESH)
-    pl.semaphore_wait(barrier, 1 + len(others))
+    for dev in neighbours + (partner,):
+        pl.semaphore_signal(barrier, inc=1, device_id=dev, device_id_type=MESH)
+    pl.semaphore_wait(barrier, 5)
 
     def remote(src, dst, ssem, rsem, dev):
         return pltpu.make_async_remote_copy(src_ref=src, dst_ref=dst, send_sem=ssem, recv_sem=rsem,
@@ -100,6 +101,10 @@
 
     issue_grad(0)
     issue_grad(1)
+    for n in range(3):
+        for dev in neighbours:
+            pl.semaphore_signal(round_sem.at[n], inc=1, device_id=dev, device_id_type=MESH)
+        pl.semaphore_wait(round_sem.at[n], 4)
     step = min(512, cols)
     out_copies = []
     tile_rows = lax.broadcasted_iota(jnp.int32, (8, 128), 0)
@@ -159,7 +164,7 @@
 
         lax.fori_loop(0, cols // step, div_step, 0)
 
-    def exchange(src_of, dst_of, dst_all, mid, hold1, hold2, ssem, msem, h1sem, h2sem, fsem):
+    def exchange(src_of, dst_of, dst_all, mid, hold1, hold2, ssem, msem, h1sem, h2sem, fsem, idle):
         sends = []
 
         def send(src, dst, rsem, dev):
@@ -167,7 +172,6 @@
             c.start()
             sends.append(c)
 
-        locals_ = []
         ways = []
         for h in range(2):
             p, q = (x, y) if h == 0 else (y, x)
@@ -190,52 +194,54 @@
         def second(h, o, piece):
             p, q, (pu, pd, pf), (qu, qd, qf), dev, src, dst = ways[h]
             start_p = (pd, pu, pf, p)[o]
+            side, i = PLACE[o]
+            send(piece(qf), hold2.at[h, side, i], h2sem.at[h, side, i], dev(p, (qu, qd)[side]))
             send(piece(qu), dst(start_p, q), fsem, dev(p, qu))
             send(piece(qd), dst(start_p, q), fsem, dev(p, qd))
-            side, i = ((0, 1), (1, 0), (1, 1), (0, 0))[o]
-            send(piece(qf), hold2.at[h, side, i], h2sem.at[h, side, i], dev(p, (qu, qd)[side]))
-            c = pltpu.make_async_copy(piece(q), dst(start_p, q), fsem)
-            c.start()
+            pltpu.make_async_copy(piece(q), dst(start_p, q), fsem).start()
 
         def relay2(h, o):
             p, q, (pu, pd, pf), (qu, qd, qf), dev, src, dst = ways[h]
-            start_p = (pd, pu, pf, p)[o]
-            side, i = ((0, 1), (1, 0), (1, 1), (0, 0))[o]
+            side, i = PLACE[o]
             held = hold2.at[h, side, i]
             pltpu.make_async_copy(held, held, h2sem.at[h, side, i]).wait()
-            send(held, dst(start_p, (qd, qu)[side]), fsem, dev(p, (qu, qd)[side]))
+            send(held, dst((pd, pu, pf, p)[o], (qd, qu)[side]), fsem, dev(p, (qu, qd)[side]))
+
+        def near_pieces(i):
+            for h in range(2):
+                p, q, (pu, pd, pf), _, dev, src, dst = ways[h]
+                for side, to in ((0, pu), (1, pd)):
+                    send(src(to, i), mid.at[h, side, i], msem.at[h, side], dev(to, q))
 
         for h in range(2):
             p, q, (pu, pd, pf), _, dev, src, dst = ways[h]
             for side, to in ((0, pu), (1, pd)):
                 for i in range(2):
                     send(src(pf, 2 * side + i), hold1.at[h, side, i], h1sem.at[h, side], dev(to, q))
-        for i in range(SIDE):
-            for h in range(2):
-                p, q, (pu, pd, pf), _, dev, src, dst = ways[h]
-                for side, to in ((0, pu), (1, pd)):
-                    send(src(to, i), mid.at[h, side, i], msem.at[h, side], dev(to, q))
-        for h in range(2):
-            second(h, 3, lambda qq, h=h: ways[h][5](ways[h][0], qq))
+        near_pieces(0)
+        near_pieces(1)
+        idle()
         for h in range(2):
             p, q, (pu, pd, pf), _, dev, src, dst = ways[h]
             for side, to in ((0, pu), (1, pd)):
                 held = hold1.at[h, side]
                 pltpu.make_async_copy(held, held, h1sem.at[h, side]).wait()
                 send(held, mid.at[h, 2, 2 * side:2 * side + 2], msem.at[h, 2 + side], dev(to, q))
+        near_pieces(2)
+        near_pieces(3)
+        for h in range(2):
+            second(h, 3, lambda qq, h=h: ways[h][5](ways[h][0], qq))
+        for h in range(2):
+            for side in range(2):
+                got = mid.at[h, 2, 2 * side:2 * side + 2]
+                pltpu.make_async_copy(got, got, msem.at[h, 2 + side]).wait()
+            second(h, 2, lambda qq, h=h: mid.at[h, 2, qq])
         for side in range(2):
             for h in range(2):
                 got = mid.at[h, side]
                 pltpu.make_async_copy(got, got, msem.at[h, side]).wait()
                 second(h, side, lambda qq, h=h, side=side: mid.at[h, side, qq])
-        for h in range(2):
-            relay2(h, 3)
-        for h in range(2):
-            for side in range(2):
-                got = mid.at[h, 2, 2 * side:2 * side + 2]
-                pltpu.make_async_copy(got, got, msem.at[h, 2 + side]).wait()
-            second(h, 2, lambda qq, h=h: mid.at[h, 2, qq])
-        for o in (0, 1, 2):
+        for o in (3, 2, 0, 1):
             for h in range(2):
                 relay2(h, o)
         pltpu.make_async_copy(dst_all, dst_all, fsem).wait()
@@ -246,10 +252,18 @@
     def piece_ds(pos, h):
         return pl.ds(pl.multiple_of(pos * quarter + h * half_piece, half_piece), half_piece)
 
+    def idle_first():
+        for k in range(n_mat):
+            for c in gcopies[k]:
+                c.wait_send()
+            out_copies[k].wait()
+        for c in [pair_copy] + norm_copies:
+            c.wait_send()
+
     my_mat, my_pos = mat_of(y, x), pos_of(y, x)
     col_copies = exchange(lambda py, px, h: xrow.at[mat_of(py, px), :, piece_ds(pos_of(py, px), h)],
                           lambda oy, ox, h: xfull.at[row_ds(ox * SIDE + oy), h * half_piece:(h + 1) * half_piece],
-                          xfull, cmid, chold1, chold2, csend, cmsem, ch1sem, ch2sem, cfsem)
+                          xfull, cmid, chold1, chold2, csend, cmsem, ch1sem, ch2sem, cfsem, idle_first)
 
     fy, fx = y + 1 - 2 * (y % 2), x + 1 - 2 * (x % 2)
     square = ((y, fx), (fy, x), (fy, fx))
@@ -280,6 +294,14 @@
         pos = my_pos if n == 0 else pos_of(*square[n - 1])
         held = agbuf.at[it, packed_ds(t, pos), :]
         return remote(held, held, fwsend.at[it, n], fwrcv.at[it, n], partner)
+
+    def drain(it):
+        pair_of(it).wait_send()
+        for n in range(3):
+            scatter_of(it, n).wait_send()
+            gather_of(it, n).wait_send()
+        for n in range(4):
+            forward_of(it, n).wait_send()
 
     def half_gram(it, h):
         nt = (((1,), (1,)), ((), ()))
@@ -301,6 +323,11 @@
         red[it] = part[it, t] + drecv[it]
         for n in range(3):
             scatter_of(it, n).start()
+
+        @pl.when(it > 0)
+        def _():
+            drain(it - 1)
+
         for n in range(3):
             scatter_of(it, n).wait_recv()
         total = (red[it, chunk_ds(my_pos), :] + rsrecv[it, 0]) + (rsrecv[it, 1] + rsrecv[it, 2])
@@ -335,30 +362,11 @@
     lax.fori_loop(0, NS_STEPS, iteration, 0)
 
     back_copies = exchange(lambda py, px, h: xfull.at[row_ds(px * SIDE + py), h * half_piece:(h + 1) * half_piece],
-                           lambda oy, ox, h: xfin.at[mat_of(oy, ox), :, piece_ds(pos_of(oy, ox), h)],
-                           xfin, bmid, bhold1, bhold2, bsend, bmsem, bh1sem, bh2sem, bfsem)
-    fin = pltpu.make_async_copy(xfin, xfin_hbm, load_sem.at[0, 0])
-    fin.start()
-
-    for k in range(n_mat):
-        for c in gcopies[k]:
-            c.wait_send()
-        out_copies[k].wait()
-    pair_copy.wait_send()
-    for c in norm_copies + back_copies:
+                           lambda oy, ox, h: xfin_hbm.at[mat_of(oy, ox), :, piece_ds(pos_of(oy, ox), h)],
+                           xfin_hbm, bmid, bhold1, bhold2, bsend, bmsem, bh1sem, bh2sem, bfsem, lambda: drain(NS_STEPS - 1))
+
+    for c in back_copies:
         c.wait_send()
-
-    def drain(it, carry):
-        pair_of(it).wait_send()
-        for n in range(3):
-            scatter_of(it, n).wait_send()
-            gather_of(it, n).wait_send()
-        for n in range(4):
-            forward_of(it, n).wait_send()
-        return carry
-
-    lax.fori_loop(0, NS_STEPS, drain, 0)
-    fin.wait()
 
 
 def run_kernel(m_blk, g_blk):
@@ -384,7 +392,6 @@
         pltpu.VMEM((n_mat, rows, cols), F32),
         pltpu.VMEM((n_mat, rows, cols), BF16),
         pltpu.VMEM((all_rows, quarter), BF16),
-        pltpu.VMEM((n_mat, rows, cols), BF16),
         pltpu.VMEM((8, 128), F32),
         pltpu.VMEM((8, 128), F32),
         pltpu.VMEM((SIDE * SIDE, 8, 128), F32),
@@ -399,7 +406,7 @@
         dma((2, n_mat)), dma((n_mat,)), dma((n_mat, 6)), dma((n_mat, 6)),
         dma((n_oth + 1,)), dma((n_oth + 1,)), *relay_sems, *relay_sems,
         dma((NS_STEPS,)), dma((NS_STEPS,)), dma((NS_STEPS, 3)), dma((NS_STEPS, 3)),
-        dma((NS_STEPS, 3)), dma((NS_STEPS, 3)), dma((NS_STEPS, 4)), dma((NS_STEPS, 4)),
+        dma((NS_STEPS, 3)), dma((NS_STEPS, 3)), dma((NS_STEPS, 4)), dma((NS_STEPS, 4)), pltpu.SemaphoreType.REGULAR((3,)),
     ]
     anyspace = pl.BlockSpec(memory_space=pl.ANY)
     return pl.pallas_call(

time: 243 us -> 240 us (0.988)
  no operation moved by 1% of the time
where the time goes in v4:
time: 240 us
  Pallas kernels  235 us (98%)
  other arithmetic  2.67 us (1%)
    pallas_call x1, Pallas kernels, run_kernel(): pl.pallas_call(muon_kernel, out_shape=(jax.ShapeDtypeStruct(m_blk.shape,...  235 us

profile of v4, /device:TPU:97, one launch (start us, length us, event | category | flops | bytes accessed | tf_op | source)
XLA Modules:
  0.0 240.3 jit_solution(9956252866192659373)
XLA Ops:
  0.6 0.0 copy-start
  0.6 235.0 %muon_group.1 = (f32[4,32,8192]{2,1,0:T(8,128)S(1)}, bf16[4,32,8192]{2,1,0:T(8,128)(2,1)S(1)}) custom-call(f32[4,32,8192]{2,1,0:T(8,128)} %m_hbm.1, bf16[4,128,8192]{2,1,0:T(8,128)(2,1)} %bitcast.1), custom_call_target="tpu_custom_call" | custom-call | tf_op jit(solution)/shard_map/muon_group/pallas_call | solution.py:412
  235.6 0.0 copy-done
  235.6 2.7 %multiply_subtract_fusion = f32[4,32,8192]{2,1,0:T(8,128)} fusion(bf16[4,32,8192]{2,1,0:T(8,128)(2,1)S(1)} %get-tuple-element.4, f32[4,32,8192]{2,1,0:T(8,128)S(1)} %copy-done), kind=kLoop, calls=%fused_computation | loop fusion | flops 4194304 | bytes 10485760 | tf_op jit(solution)/shard_map/sub | solution.py:433
  238.3 2.0 copy.6
Async XLA Ops:
  0.6 235.0 %copy-start = (f32[4,32,8192]{2,1,0:T(8,128)S(1)}, f32[4,32,8192]{2,1,0:T(8,128)}, u32[]{:S(2)}) copy-start(f32[4,32,8192]{2,1,0:T(8,128)} %param.3) | copy-start | bytes 12582916

commit v5 on v4

--- a/solution.py
+++ b/solution.py
@@ -29,7 +29,7 @@
 
 def muon_kernel(m_hbm, g_hbm, mnew_hbm, xfin_hbm,
                 gown, grecv, relay, mbuf, x0, xrow, xfull,
-                nown, npair, nall, part, drecv, red, rsrecv, agbuf, amat, bmat,
+                nown, npair, nall, part, drecv, red, comb, rsrecv, agbuf, amat, bmat,
                 cmid, chold1, chold2, bmid, bhold1, bhold2,
                 load_sem, out_sem, gsend, grcv, nsend, nrcv, csend, cmsem, ch1sem, ch2sem, cfsem,
                 bsend, bmsem, bh1sem, bh2sem, bfsem,
@@ -109,19 +109,14 @@
     out_copies = []
     tile_rows = lax.broadcasted_iota(jnp.int32, (8, 128), 0)
     norm_tile = jnp.zeros((8, 128), F32)
-    for k in range(n_mat):
-        gcopies[k][2].wait_recv()
-        gcopies[k][4].start()
-        gcopies[k][3].wait_recv()
-        gcopies[k][5].start()
-        if k + 2 < n_mat:
-            issue_grad(k + 2)
+
+    def momentum_step(k, norm_tile):
         for c in loads[k]:
             c.wait()
         for j in (0, 1, 4, 5):
             gcopies[k][j].wait_recv()
 
-        def col_step(i, acc, k=k):
+        def col_step(i, acc):
             cs = pl.ds(pl.multiple_of(i * step, step), step)
             g_sum = (gown[k, :, cs].astype(F32) + grecv[k, 0, :, cs].astype(F32)) + (
                 grecv[k, 1, :, cs].astype(F32) + grecv[k, 2, :, cs].astype(F32))
@@ -132,10 +127,20 @@
             return acc + x_zero * x_zero
 
         acc = lax.fori_loop(0, cols // step, col_step, jnp.zeros((rows, step), F32))
-        norm_tile = jnp.where(tile_rows == k, jnp.sum(acc), norm_tile)
         oc = pltpu.make_async_copy(mbuf.at[k], mnew_hbm.at[k], out_sem.at[k])
         oc.start()
         out_copies.append(oc)
+        return jnp.where(tile_rows == k, jnp.sum(acc), norm_tile)
+
+    for k in range(n_mat):
+        for j in (2, 3):
+            gcopies[k][j].wait_recv()
+            gcopies[k][j + 2].start()
+        if k + 2 < n_mat:
+            issue_grad(k + 2)
+        if k > 0:
+            norm_tile = momentum_step(k - 1, norm_tile)
+    norm_tile = momentum_step(n_mat - 1, norm_tile)
 
     nown[...] = norm_tile
     pair_copy = remote(nown, npair, nsend.at[0], nrcv.at[0], partner)
@@ -277,13 +282,23 @@
 
     bcol = min(256, quarter)
 
-    def pair_of(it):
-        return remote(part.at[it, 1 - t], drecv.at[it], dsend.at[it], drcv.at[it], partner)
-
-    def scatter_of(it, n):
-        py, px = square[n]
-        return remote(red.at[it, chunk_ds(pos_of(py, px)), :], rsrecv.at[it, n], rssend.at[it, n], rsrcv.at[it, n],
-                      {'dp': py, 'fsdp': px})
+    near_x, near_y, diagonal = (pos_of(*c) for c in square)
+    to_x, to_y = {'fsdp': fx}, {'dp': fy}
+    sub = chunk // 2
+
+    def sub_ds(pos, h):
+        return pl.ds(pl.multiple_of(pos * chunk + h * sub, sub), sub)
+
+    def pair_of(it, n):
+        cs = chunk_ds((diagonal, near_x, near_y, my_pos)[n])
+        return remote(part.at[it, 1 - t, cs, :], drecv.at[it, cs, :], dsend.at[it, n], drcv.at[it, n], partner)
+
+    def reduce_of(it, n):
+        src = (red.at[it, sub_ds(diagonal, 0), :], red.at[it, sub_ds(diagonal, 1), :],
+               red.at[it, sub_ds(near_x, 0), :], red.at[it, sub_ds(near_y, 1), :],
+               comb.at[it, 0], comb.at[it, 1])[n]
+        to = (to_x, to_y, to_x, to_y, to_y, to_x)[n]
+        return remote(src, rsrecv.at[it, n], rssend.at[it, n], rsrcv.at[it, n], to)
 
     def gather_of(it, n):
         mine = agbuf.at[it, packed_ds(t, my_pos), :]
@@ -296,12 +311,13 @@
         return remote(held, held, fwsend.at[it, n], fwrcv.at[it, n], partner)
 
     def drain(it):
-        pair_of(it).wait_send()
+        for n in range(4):
+            pair_of(it, n).wait_send()
+            forward_of(it, n).wait_send()
+        for n in range(6):
+            reduce_of(it, n).wait_send()
         for n in range(3):
-            scatter_of(it, n).wait_send()
             gather_of(it, n).wait_send()
-        for n in range(4):
-            forward_of(it, n).wait_send()
 
     def half_gram(it, h):
         nt = (((1,), (1,)), ((), ()))
@@ -316,23 +332,33 @@
 
     def iteration(it, carry):
         half_gram(it, 1 - t)
-        pair = pair_of(it)
-        pair.start()
+        for n in range(4):
+            pair_of(it, n).start()
         half_gram(it, t)
-        pair.wait_recv()
-        red[it] = part[it, t] + drecv[it]
-        for n in range(3):
-            scatter_of(it, n).start()
+        for n, pos in enumerate((diagonal, near_x, near_y, my_pos)):
+            pair_of(it, n).wait_recv()
+            cs = chunk_ds(pos)
+            red[it, cs, :] = part[it, t, cs, :] + drecv[it, cs, :]
+            for m in ((0, 1), (2,), (3,), ())[n]:
+                reduce_of(it, m).start()
+        reduce_of(it, 0).wait_recv()
+        comb[it, 0] = red[it, sub_ds(near_y, 0), :] + rsrecv[it, 0]
+        reduce_of(it, 4).start()
+        reduce_of(it, 1).wait_recv()
+        comb[it, 1] = red[it, sub_ds(near_x, 1), :] + rsrecv[it, 1]
+        reduce_of(it, 5).start()
 
         @pl.when(it > 0)
         def _():
             drain(it - 1)
 
-        for n in range(3):
-            scatter_of(it, n).wait_recv()
-        total = (red[it, chunk_ds(my_pos), :] + rsrecv[it, 0]) + (rsrecv[it, 1] + rsrecv[it, 2])
-        agbuf[it, packed_ds(t, my_pos), :] = total.astype(BF16)
-        for n in range(3):
+        for h in range(2):
+            reduce_of(it, 2 + h).wait_recv()
+            reduce_of(it, 4 + h).wait_recv()
+            total = (red[it, sub_ds(my_pos, h), :] + rsrecv[it, 2 + h]) + rsrecv[it, 4 + h]
+            mine = pl.ds(pl.multiple_of(t * (HALF * BLK) + my_pos * chunk + h * sub, sub), sub)
+            agbuf[it, mine, :] = total.astype(BF16)
+        for n in (2, 0, 1):
             gather_of(it, n).start()
         forward_of(it, 0).start()
         for n in range(3):
@@ -398,14 +424,15 @@
         pltpu.VMEM((NS_STEPS, 2, packed // 2, BLK), F32),
         pltpu.VMEM((NS_STEPS, packed // 2, BLK), F32),
         pltpu.VMEM((NS_STEPS, packed // 2, BLK), F32),
-        pltpu.VMEM((NS_STEPS, 3, chunk, BLK), F32),
+        pltpu.VMEM((NS_STEPS, 2, chunk // 2, BLK), F32),
+        pltpu.VMEM((NS_STEPS, 6, chunk // 2, BLK), F32),
         pltpu.VMEM((NS_STEPS, packed, BLK), BF16),
         pltpu.VMEM((all_rows, all_rows), BF16),
         pltpu.VMEM((all_rows, all_rows), BF16),
         *relays, *relays,
         dma((2, n_mat)), dma((n_mat,)), dma((n_mat, 6)), dma((n_mat, 6)),
         dma((n_oth + 1,)), dma((n_oth + 1,)), *relay_sems, *relay_sems,
-        dma((NS_STEPS,)), dma((NS_STEPS,)), dma((NS_STEPS, 3)), dma((NS_STEPS, 3)),
+        dma((NS_STEPS, 4)), dma((NS_STEPS, 4)), dma((NS_STEPS, 6)), dma((NS_STEPS, 6)),
         dma((NS_STEPS, 3)), dma((NS_STEPS, 3)), dma((NS_STEPS, 4)), dma((NS_STEPS, 4)), pltpu.SemaphoreType.REGULAR((3,)),
     ]
     anyspace = pl.BlockSpec(memory_space=pl.ANY)

time: 240 us -> 239 us (level)
  no operation moved by 1% of the time
where the time goes in v5:
time: 239 us
  Pallas kernels  233 us (97%)
  other arithmetic  2.67 us (1%)
    pallas_call x1, Pallas kernels, run_kernel(): pl.pallas_call(muon_kernel, out_shape=(jax.ShapeDtypeStruct(m_blk.shape,...  233 us

profile of v5, /device:TPU:97, one launch (start us, length us, event | category | flops | bytes accessed | tf_op | source)
XLA Modules:
  0.0 238.5 jit_solution(13602768287649938649)
XLA Ops:
  0.6 0.0 copy-start
  0.6 233.2 %muon_group.1 = (f32[4,32,8192]{2,1,0:T(8,128)S(1)}, bf16[4,32,8192]{2,1,0:T(8,128)(2,1)S(1)}) custom-call(f32[4,32,8192]{2,1,0:T(8,128)} %m_hbm.1, bf16[4,128,8192]{2,1,0:T(8,128)(2,1)} %bitcast.1), custom_call_target="tpu_custom_call" | custom-call | tf_op jit(solution)/shard_map/muon_group/pallas_call | solution.py:439
  233.8 0.0 copy-done
  233.8 2.7 %multiply_subtract_fusion = f32[4,32,8192]{2,1,0:T(8,128)} fusion(bf16[4,32,8192]{2,1,0:T(8,128)(2,1)S(1)} %get-tuple-element.4, f32[4,32,8192]{2,1,0:T(8,128)S(1)} %copy-done), kind=kLoop, calls=%fused_computation | loop fusion | flops 4194304 | bytes 10485760 | tf_op jit(solution)/shard_map/sub | solution.py:460
  236.5 2.0 copy.6
Async XLA Ops:
  0.6 233.2 %copy-start = (f32[4,32,8192]{2,1,0:T(8,128)S(1)}, f32[4,32,8192]{2,1,0:T(8,128)}, u32[]{:S(2)}) copy-start(f32[4,32,8192]{2,1,0:T(8,128)} %param.3) | copy-start | bytes 12582916

commit v6 on v5

--- a/solution.py
+++ b/solution.py
@@ -29,7 +29,7 @@
 
 def muon_kernel(m_hbm, g_hbm, mnew_hbm, xfin_hbm,
                 gown, grecv, relay, mbuf, x0, xrow, xfull,
-                nown, npair, nall, part, drecv, red, comb, rsrecv, agbuf, amat, bmat,
+                nown, npair, nall, part, drecv, comb, rsrecv, agbuf, amat, bmat,
                 cmid, chold1, chold2, bmid, bhold1, bhold2,
                 load_sem, out_sem, gsend, grcv, nsend, nrcv, csend, cmsem, ch1sem, ch2sem, cfsem,
                 bsend, bmsem, bh1sem, bh2sem, bfsem,
@@ -272,13 +272,11 @@
 
     fy, fx = y + 1 - 2 * (y % 2), x + 1 - 2 * (x % 2)
     square = ((y, fx), (fy, x), (fy, fx))
-    chunk = HALF * BLK // 4
+    packed = len(TRI) * BLK
+    chunk = packed // 4
 
     def chunk_ds(pos):
         return pl.ds(pl.multiple_of(pos * chunk, chunk), chunk)
-
-    def packed_ds(core, pos):
-        return pl.ds(pl.multiple_of(core * (HALF * BLK) + pos * chunk, chunk), chunk)
 
     bcol = min(256, quarter)
 
@@ -289,83 +287,103 @@
     def sub_ds(pos, h):
         return pl.ds(pl.multiple_of(pos * chunk + h * sub, sub), sub)
 
+    pieces = [slice(h * HALF * BLK + lo_ * BLK, h * HALF * BLK + hi_ * BLK) for h in range(2) for lo_, hi_ in ((0, 3), (3, HALF))]
+
     def pair_of(it, n):
-        cs = chunk_ds((diagonal, near_x, near_y, my_pos)[n])
-        return remote(part.at[it, 1 - t, cs, :], drecv.at[it, cs, :], dsend.at[it, n], drcv.at[it, n], partner)
+        return remote(part.at[it, pieces[n], :], drecv.at[it, pieces[n], :], dsend.at[it, n], drcv.at[it, n], partner)
 
     def reduce_of(it, n):
-        src = (red.at[it, sub_ds(diagonal, 0), :], red.at[it, sub_ds(diagonal, 1), :],
-               red.at[it, sub_ds(near_x, 0), :], red.at[it, sub_ds(near_y, 1), :],
+        src = (part.at[it, sub_ds(diagonal, 0), :], part.at[it, sub_ds(diagonal, 1), :],
+               part.at[it, sub_ds(near_x, 0), :], part.at[it, sub_ds(near_y, 1), :],
                comb.at[it, 0], comb.at[it, 1])[n]
         to = (to_x, to_y, to_x, to_y, to_y, to_x)[n]
         return remote(src, rsrecv.at[it, n], rssend.at[it, n], rsrcv.at[it, n], to)
 
     def gather_of(it, n):
-        mine = agbuf.at[it, packed_ds(t, my_pos), :]
+        mine = agbuf.at[it, chunk_ds(my_pos), :]
         py, px = square[n]
         return remote(mine, mine, agsend.at[it, n], agrcv.at[it, n], {'dp': py, 'fsdp': px})
 
     def forward_of(it, n):
         pos = my_pos if n == 0 else pos_of(*square[n - 1])
-        held = agbuf.at[it, packed_ds(t, pos), :]
+        held = agbuf.at[it, chunk_ds(pos), :]
         return remote(held, held, fwsend.at[it, n], fwrcv.at[it, n], partner)
 
+    leads = t == 1
+
     def drain(it):
+        @pl.when(leads)
+        def _():
+            for n in range(6):
+                reduce_of(it, n).wait_send()
+            for n in range(3):
+                gather_of(it, n).wait_send()
+            for n in range(4):
+                forward_of(it, n).wait_send()
+
+        @pl.when(t == 0)
+        def _():
+            for n in range(4):
+                pair_of(it, n).wait_send()
+
+    def gram_piece(it, n):
+        nt = (((1,), (1,)), ((), ()))
+        h = n // 2
+        if n % 2 == 0:
+            pair_rows = xfull[2 * BLK * h:2 * BLK * (h + 1), :]
+            gram = lax.dot_general(pair_rows, pair_rows, nt, preferred_element_type=F32)
+            blocks = (gram[:BLK, :BLK], gram[:BLK, BLK:], gram[BLK:, BLK:])
+        else:
+            gram = lax.dot_general(xfull[h * BLK:(h + 1) * BLK, :], xfull[2 * BLK:, :], nt, preferred_element_type=F32)
+            blocks = (gram[:, :BLK], gram[:, BLK:])
+        for i, block in enumerate(blocks):
+            part[it, pieces[n].start + i * BLK:pieces[n].start + (i + 1) * BLK, :] = block
+
+    def lead(it):
         for n in range(4):
-            pair_of(it, n).wait_send()
-            forward_of(it, n).wait_send()
-        for n in range(6):
-            reduce_of(it, n).wait_send()
-        for n in range(3):
-            gather_of(it, n).wait_send()
-
-    def half_gram(it, h):
-        nt = (((1,), (1,)), ((), ()))
-        pair_rows = xfull[pl.ds(pl.multiple_of(h * 2 * BLK, 2 * BLK), 2 * BLK), :]
-        square_gram = lax.dot_general(pair_rows, pair_rows, nt, preferred_element_type=F32)
-        cross_gram = lax.dot_general(xfull[pl.ds(pl.multiple_of(h * BLK, BLK), BLK), :], xfull[2 * BLK:, :], nt,
-                                     preferred_element_type=F32)
-        blocks = (square_gram[:BLK, :BLK], square_gram[:BLK, BLK:], square_gram[BLK:, BLK:],
-                  cross_gram[:, :BLK], cross_gram[:, BLK:])
-        for n, block in enumerate(blocks):
-            part[it, h, n * BLK:(n + 1) * BLK, :] = block
-
-    def iteration(it, carry):
-        half_gram(it, 1 - t)
+            pair_of(it, n).wait_recv()
+            part[it, pieces[n], :] += drecv[it, pieces[n], :]
         for n in range(4):
-            pair_of(it, n).start()
-        half_gram(it, t)
-        for n, pos in enumerate((diagonal, near_x, near_y, my_pos)):
-            pair_of(it, n).wait_recv()
-            cs = chunk_ds(pos)
-            red[it, cs, :] = part[it, t, cs, :] + drecv[it, cs, :]
-            for m in ((0, 1), (2,), (3,), ())[n]:
-                reduce_of(it, m).start()
+            reduce_of(it, n).start()
         reduce_of(it, 0).wait_recv()
-        comb[it, 0] = red[it, sub_ds(near_y, 0), :] + rsrecv[it, 0]
+        comb[it, 0] = part[it, sub_ds(near_y, 0), :] + rsrecv[it, 0]
         reduce_of(it, 4).start()
         reduce_of(it, 1).wait_recv()
-        comb[it, 1] = red[it, sub_ds(near_x, 1), :] + rsrecv[it, 1]
+        comb[it, 1] = part[it, sub_ds(near_x, 1), :] + rsrecv[it, 1]
         reduce_of(it, 5).start()
-
-        @pl.when(it > 0)
-        def _():
-            drain(it - 1)
-
         for h in range(2):
             reduce_of(it, 2 + h).wait_recv()
             reduce_of(it, 4 + h).wait_recv()
-            total = (red[it, sub_ds(my_pos, h), :] + rsrecv[it, 2 + h]) + rsrecv[it, 4 + h]
-            mine = pl.ds(pl.multiple_of(t * (HALF * BLK) + my_pos * chunk + h * sub, sub), sub)
-            agbuf[it, mine, :] = total.astype(BF16)
+            total = (part[it, sub_ds(my_pos, h), :] + rsrecv[it, 2 + h]) + rsrecv[it, 4 + h]
+            agbuf[it, sub_ds(my_pos, h), :] = total.astype(BF16)
         for n in (2, 0, 1):
             gather_of(it, n).start()
         forward_of(it, 0).start()
         for n in range(3):
             gather_of(it, n).wait_recv()
             forward_of(it, n + 1).start()
+
+    def iteration(it, carry):
         for n in range(4):
-            forward_of(it, n).wait_recv()
+            gram_piece(it, n)
+
+            @pl.when(t == 0)
+            def _(n=n):
+                pair_of(it, n).start()
+
+        @pl.when(it > 0)
+        def _():
+            drain(it - 1)
+
+        @pl.when(leads)
+        def _():
+            lead(it)
+
+        @pl.when(t == 0)
+        def _():
+            for n in range(4):
+                forward_of(it, n).wait_recv()
+
         for n, (bi, bj) in enumerate(TRI):
             block = agbuf[it, n * BLK:(n + 1) * BLK, :]
             amat[bi * BLK:(bi + 1) * BLK, bj * BLK:(bj + 1) * BLK] = block
@@ -400,7 +418,7 @@
     all_rows = rows * SIDE * SIDE
     quarter = cols // SIDE
     packed = len(TRI) * BLK
-    chunk = packed // 8
+    chunk = packed // 4
     n_oth = SIDE * SIDE - 1
     dma = pltpu.SemaphoreType.DMA
     half_piece = (rows, quarter // 2)
@@ -421,9 +439,8 @@
         pltpu.VMEM((8, 128), F32),
         pltpu.VMEM((8, 128), F32),
         pltpu.VMEM((SIDE * SIDE, 8, 128), F32),
-        pltpu.VMEM((NS_STEPS, 2, packed // 2, BLK), F32),
-        pltpu.VMEM((NS_STEPS, packed // 2, BLK), F32),
-        pltpu.VMEM((NS_STEPS, packed // 2, BLK), F32),
+        pltpu.VMEM((NS_STEPS, packed, BLK), F32),
+        pltpu.VMEM((NS_STEPS, packed, BLK), F32),
         pltpu.VMEM((NS_STEPS, 2, chunk // 2, BLK), F32),
         pltpu.VMEM((NS_STEPS, 6, chunk // 2, BLK), F32),
         pltpu.VMEM((NS_STEPS, packed, BLK), BF16),

time: 239 us -> 243 us (1.017)
  Pallas kernels: 233 us -> 237 us
    pallas_call x1, Pallas kernels: 233 us -> 237 us  [run_kernel(): pl.pallas_call(muon_kernel, out_shape=(jax.ShapeDtypeStruct(m_blk.shape,...]
where the time goes in v6:
time: 243 us; the launch traced here: 242 us
  Pallas kernels  237 us (98%)
  other arithmetic  2.67 us (1%)
    pallas_call x1, Pallas kernels, run_kernel(): pl.pallas_call(muon_kernel, out_shape=(jax.ShapeDtypeStruct(m_blk.shape,...  237 us

profile of v6, /device:TPU:97, one launch (start us, length us, event | category | flops | bytes accessed | tf_op | source)
XLA Modules:
  0.0 242.1 jit_solution(5025061641660373290)
XLA Ops:
  0.6 0.0 copy-start
  0.6 236.7 %muon_group.1 = (f32[4,32,8192]{2,1,0:T(8,128)S(1)}, bf16[4,32,8192]{2,1,0:T(8,128)(2,1)S(1)}) custom-call(f32[4,32,8192]{2,1,0:T(8,128)} %m_hbm.1, bf16[4,128,8192]{2,1,0:T(8,128)(2,1)} %bitcast.1), custom_call_target="tpu_custom_call" | custom-call | tf_op jit(solution)/shard_map/muon_group/pallas_call | solution.py:456
  237.4 0.0 copy-done
  237.4 2.7 %multiply_subtract_fusion = f32[4,32,8192]{2,1,0:T(8,128)} fusion(bf16[4,32,8192]{2,1,0:T(8,128)(2,1)S(1)} %get-tuple-element.4, f32[4,32,8192]{2,1,0:T(8,128)S(1)} %copy-done), kind=kLoop, calls=%fused_computation | loop fusion | flops 4194304 | bytes 10485760 | tf_op jit(solution)/shard_map/sub | solution.py:477
  240.1 2.0 copy.6
Async XLA Ops:
  0.6 236.7 %copy-start = (f32[4,32,8192]{2,1,0:T(8,128)S(1)}, f32[4,32,8192]{2,1,0:T(8,128)}, u32[]{:S(2)}) copy-start(f32[4,32,8192]{2,1,0:T(8,128)} %param.3) | copy-start | bytes 12582916

commit v7 on v5

--- a/solution.py
+++ b/solution.py
@@ -19,7 +19,7 @@
 F32 = jnp.float32
 BF16 = jnp.bfloat16
 MESH = pl.DeviceIdType.MESH
-VMEM_MIB = 47
+VMEM_MIB = 46
 SIDE = 4
 BLK = 128
 TRI = ((0, 0), (0, 1), (1, 1), (0, 2), (0, 3), (2, 2), (2, 3), (3, 3), (1, 2), (1, 3))
@@ -132,42 +132,34 @@
         out_copies.append(oc)
         return jnp.where(tile_rows == k, jnp.sum(acc), norm_tile)
 
-    for k in range(n_mat):
-        for j in (2, 3):
-            gcopies[k][j].wait_recv()
-            gcopies[k][j + 2].start()
-        if k + 2 < n_mat:
-            issue_grad(k + 2)
-        if k > 0:
-            norm_tile = momentum_step(k - 1, norm_tile)
-    norm_tile = momentum_step(n_mat - 1, norm_tile)
-
-    nown[...] = norm_tile
-    pair_copy = remote(nown, npair, nsend.at[0], nrcv.at[0], partner)
-    pair_copy.start()
-    pair_copy.wait_recv()
+    norm_copies = []
     here = y * SIDE + x
-    nall[here] = nown[...] + npair[...]
-    norm_copies = []
-    for n, off in enumerate(others):
-        py, px = peer(off)
-        c = remote(nall.at[here], nall.at[here], nsend.at[1 + n], nrcv.at[1 + n], {'dp': py, 'fsdp': px})
-        c.start()
-        norm_copies.append(c)
-    for c in norm_copies:
-        c.wait_recv()
-    sq_all = jnp.sum(nall[...], axis=0)
-    denom_all = jnp.sqrt(sq_all) + NORM_EPS
-
-    for k in range(n_mat):
-        denom = denom_all[k:k + 1, 0:1]
-
-        def div_step(i, carry, k=k, denom=denom):
-            cs = pl.ds(pl.multiple_of(i * step, step), step)
-            xrow[k, :, cs] = (x0[k, :, cs] / denom).astype(BF16)
-            return carry
-
-        lax.fori_loop(0, cols // step, div_step, 0)
+
+    def normalise(r, mats, tile):
+        nown[r] = tile
+        pair_copy = remote(nown.at[r], npair.at[r], nsend.at[r, 0], nrcv.at[r, 0], partner)
+        pair_copy.start()
+        pair_copy.wait_recv()
+        nall[r, here] = nown[r] + npair[r]
+        copies = []
+        for n, off in enumerate(others):
+            py, px = peer(off)
+            c = remote(nall.at[r, here], nall.at[r, here], nsend.at[r, 1 + n], nrcv.at[r, 1 + n], {'dp': py, 'fsdp': px})
+            c.start()
+            copies.append(c)
+        for c in copies:
+            c.wait_recv()
+        norm_copies.extend(copies + [pair_copy])
+        denom_all = jnp.sqrt(jnp.sum(nall[r], axis=0)) + NORM_EPS
+        for k in mats:
+            denom = denom_all[k:k + 1, 0:1]
+
+            def div_step(i, carry, k=k, denom=denom):
+                cs = pl.ds(pl.multiple_of(i * step, step), step)
+                xrow[k, :, cs] = (x0[k, :, cs] / denom).astype(BF16)
+                return carry
+
+            lax.fori_loop(0, cols // step, div_step, 0)
 
     def exchange(src_of, dst_of, dst_all, mid, hold1, hold2, ssem, msem, h1sem, h2sem, fsem, idle):
         sends = []
@@ -218,13 +210,17 @@
                 for side, to in ((0, pu), (1, pd)):
                     send(src(to, i), mid.at[h, side, i], msem.at[h, side], dev(to, q))
 
-        for h in range(2):
-            p, q, (pu, pd, pf), _, dev, src, dst = ways[h]
-            for side, to in ((0, pu), (1, pd)):
-                for i in range(2):
-                    send(src(pf, 2 * side + i), hold1.at[h, side, i], h1sem.at[h, side], dev(to, q))
+        def far_pieces(i):
+            for h in range(2):
+                p, q, (pu, pd, pf), _, dev, src, dst = ways[h]
+                for side, to in ((0, pu), (1, pd)):
+                    send(src(pf, 2 * i + side), hold1.at[h, side, i], h1sem.at[h, side], dev(to, q))
+
+        far_pieces(0)
         near_pieces(0)
         near_pieces(1)
+        yield None
+        far_pieces(1)
         idle()
         for h in range(2):
             p, q, (pu, pd, pf), _, dev, src, dst = ways[h]
@@ -240,7 +236,7 @@
             for side in range(2):
                 got = mid.at[h, 2, 2 * side:2 * side + 2]
                 pltpu.make_async_copy(got, got, msem.at[h, 2 + side]).wait()
-            second(h, 2, lambda qq, h=h: mid.at[h, 2, qq])
+            second(h, 2, lambda qq, h=h: mid.at[h, 2, (qq % 2) * 2 + qq // 2])
         for side in range(2):
             for h in range(2):
                 got = mid.at[h, side]
@@ -250,7 +246,7 @@
             for h in range(2):
                 relay2(h, o)
         pltpu.make_async_copy(dst_all, dst_all, fsem).wait()
-        return sends
+        yield sends
 
     half_piece = quarter // 2
 
@@ -262,13 +258,26 @@
             for c in gcopies[k]:
                 c.wait_send()
             out_copies[k].wait()
-        for c in [pair_copy] + norm_copies:
+        for c in norm_copies:
             c.wait_send()
 
     my_mat, my_pos = mat_of(y, x), pos_of(y, x)
-    col_copies = exchange(lambda py, px, h: xrow.at[mat_of(py, px), :, piece_ds(pos_of(py, px), h)],
+    to_columns = exchange(lambda py, px, h: xrow.at[mat_of(py, px), :, piece_ds(pos_of(py, px), h)],
                           lambda oy, ox, h: xfull.at[row_ds(ox * SIDE + oy), h * half_piece:(h + 1) * half_piece],
                           xfull, cmid, chold1, chold2, csend, cmsem, ch1sem, ch2sem, cfsem, idle_first)
+    for k in range(n_mat):
+        for j in (2, 3):
+            gcopies[k][j].wait_recv()
+            gcopies[k][j + 2].start()
+        if k + 2 < n_mat:
+            issue_grad(k + 2)
+        if k > 0:
+            norm_tile = momentum_step(k - 1, norm_tile)
+    normalise(0, range(n_mat - 1), norm_tile)
+    next(to_columns)
+    normalise(1, range(n_mat - 1, n_mat), momentum_step(n_mat - 1, norm_tile))
+    col_copies = next(to_columns)
+
 
     fy, fx = y + 1 - 2 * (y % 2), x + 1 - 2 * (x % 2)
     square = ((y, fx), (fy, x), (fy, fx))
@@ -387,9 +396,11 @@
         c.wait_send()
     lax.fori_loop(0, NS_STEPS, iteration, 0)
 
-    back_copies = exchange(lambda py, px, h: xfull.at[row_ds(px * SIDE + py), h * half_piece:(h + 1) * half_piece],
+    to_rows = exchange(lambda py, px, h: xfull.at[row_ds(px * SIDE + py), h * half_piece:(h + 1) * half_piece],
                            lambda oy, ox, h: xfin_hbm.at[mat_of(oy, ox), :, piece_ds(pos_of(oy, ox), h)],
                            xfin_hbm, bmid, bhold1, bhold2, bsend, bmsem, bh1sem, bh2sem, bfsem, lambda: drain(NS_STEPS - 1))
+    next(to_rows)
+    back_copies = next(to_rows)
 
     for c in back_copies:
         c.wait_send()
@@ -418,9 +429,9 @@
         pltpu.VMEM((n_mat, rows, cols), F32),
         pltpu.VMEM((n_mat, rows, cols), BF16),
         pltpu.VMEM((all_rows, quarter), BF16),
-        pltpu.VMEM((8, 128), F32),
-        pltpu.VMEM((8, 128), F32),
-        pltpu.VMEM((SIDE * SIDE, 8, 128), F32),
+        pltpu.VMEM((2, 8, 128), F32),
+        pltpu.VMEM((2, 8, 128), F32),
+        pltpu.VMEM((2, SIDE * SIDE, 8, 128), F32),
         pltpu.VMEM((NS_STEPS, 2, packed // 2, BLK), F32),
         pltpu.VMEM((NS_STEPS, packed // 2, BLK), F32),
         pltpu.VMEM((NS_STEPS, packed // 2, BLK), F32),
@@ -431,7 +442,7 @@
         pltpu.VMEM((all_rows, all_rows), BF16),
         *relays, *relays,
         dma((2, n_mat)), dma((n_mat,)), dma((n_mat, 6)), dma((n_mat, 6)),
-        dma((n_oth + 1,)), dma((n_oth + 1,)), *relay_sems, *relay_sems,
+        dma((2, n_oth + 1)), dma((2, n_oth + 1)), *relay_sems, *relay_sems,
         dma((NS_STEPS, 4)), dma((NS_STEPS, 4)), dma((NS_STEPS, 6)), dma((NS_STEPS, 6)),
         dma((NS_STEPS, 3)), dma((NS_STEPS, 3)), dma((NS_STEPS, 4)), dma((NS_STEPS, 4)), pltpu.SemaphoreType.REGULAR((3,)),
     ]

time: 239 us -> 244 us (1.021)
  Pallas kernels: 233 us -> 238 us
    pallas_call x1, Pallas kernels: 233 us -> 238 us  [run_kernel(): pl.pallas_call(muon_kernel, out_shape=(jax.ShapeDtypeStruct(m_blk.shape,...]
where the time goes in v7:
time: 244 us; the launch traced here: 243 us
  Pallas kernels  238 us (98%)
  other arithmetic  2.67 us (1%)
    pallas_call x1, Pallas kernels, run_kernel(): pl.pallas_call(muon_kernel, out_shape=(jax.ShapeDtypeStruct(m_blk.shape,...  238 us

profile of v7, /device:TPU:97, one launch (start us, length us, event | category | flops | bytes accessed | tf_op | source)
XLA Modules:
  0.0 243.5 jit_solution(8743569671208767244)
XLA Ops:
  0.6 0.0 copy-start
  0.6 238.1 %muon_group.1 = (f32[4,32,8192]{2,1,0:T(8,128)S(1)}, bf16[4,32,8192]{2,1,0:T(8,128)(2,1)S(1)}) custom-call(f32[4,32,8192]{2,1,0:T(8,128)} %m_hbm.1, bf16[4,128,8192]{2,1,0:T(8,128)(2,1)} %bitcast.1), custom_call_target="tpu_custom_call" | custom-call | tf_op jit(solution)/shard_map/muon_group/pallas_call | solution.py:450
  238.8 0.0 copy-done
  238.8 2.7 %multiply_subtract_fusion = f32[4,32,8192]{2,1,0:T(8,128)} fusion(bf16[4,32,8192]{2,1,0:T(8,128)(2,1)S(1)} %get-tuple-element.4, f32[4,32,8192]{2,1,0:T(8,128)S(1)} %copy-done), kind=kLoop, calls=%fused_computation | loop fusion | flops 4194304 | bytes 10485760 | tf_op jit(solution)/shard_map/sub | solution.py:471
  241.4 2.0 copy.6
Async XLA Ops:
  0.6 238.1 %copy-start = (f32[4,32,8192]{2,1,0:T(8,128)S(1)}, f32[4,32,8192]{2,1,0:T(8,128)}, u32[]{:S(2)}) copy-start(f32[4,32,8192]{2,1,0:T(8,128)} %param.3) | copy-start | bytes 12582916

commit v8 on v5

--- a/solution.py
+++ b/solution.py
@@ -289,9 +289,8 @@
     def sub_ds(pos, h):
         return pl.ds(pl.multiple_of(pos * chunk + h * sub, sub), sub)
 
-    def pair_of(it, n):
-        cs = chunk_ds((diagonal, near_x, near_y, my_pos)[n])
-        return remote(part.at[it, 1 - t, cs, :], drecv.at[it, cs, :], dsend.at[it, n], drcv.at[it, n], partner)
+    def pair_of(it):
+        return remote(part.at[it, 1 - t], drecv.at[it], dsend.at[it], drcv.at[it], partner)
 
     def reduce_of(it, n):
         src = (red.at[it, sub_ds(diagonal, 0), :], red.at[it, sub_ds(diagonal, 1), :],
@@ -311,8 +310,8 @@
         return remote(held, held, fwsend.at[it, n], fwrcv.at[it, n], partner)
 
     def drain(it):
+        pair_of(it).wait_send()
         for n in range(4):
-            pair_of(it, n).wait_send()
             forward_of(it, n).wait_send()
         for n in range(6):
             reduce_of(it, n).wait_send()
@@ -332,11 +331,10 @@
 
     def iteration(it, carry):
         half_gram(it, 1 - t)
-        for n in range(4):
-            pair_of(it, n).start()
+        pair_of(it).start()
         half_gram(it, t)
+        pair_of(it).wait_recv()
         for n, pos in enumerate((diagonal, near_x, near_y, my_pos)):
-            pair_of(it, n).wait_recv()
             cs = chunk_ds(pos)
             red[it, cs, :] = part[it, t, cs, :] + drecv[it, cs, :]
             for m in ((0, 1), (2,), (3,), ())[n]:
@@ -432,7 +430,7 @@
         *relays, *relays,
         dma((2, n_mat)), dma((n_mat,)), dma((n_mat, 6)), dma((n_mat, 6)),
         dma((n_oth + 1,)), dma((n_oth + 1,)), *relay_sems, *relay_sems,
-        dma((NS_STEPS, 4)), dma((NS_STEPS, 4)), dma((NS_STEPS, 6)), dma((NS_STEPS, 6)),
+        dma((NS_STEPS,)), dma((NS_STEPS,)), dma((NS_STEPS, 6)), dma((NS_STEPS, 6)),
         dma((NS_STEPS, 3)), dma((NS_STEPS, 3)), dma((NS_STEPS, 4)), dma((NS_STEPS, 4)), pltpu.SemaphoreType.REGULAR((3,)),
     ]
     anyspace = pl.BlockSpec(memory_space=pl.ANY)

time: 239 us -> 240 us (level)
  no operation moved by 1% of the time
where the time goes in v8:
time: 240 us
  Pallas kernels  234 us (98%)
  other arithmetic  2.67 us (1%)
    pallas_call x1, Pallas kernels, run_kernel(): pl.pallas_call(muon_kernel, out_shape=(jax.ShapeDtypeStruct(m_blk.shape,...  234 us

profile of v8, /device:TPU:97, one launch (start us, length us, event | category | flops | bytes accessed | tf_op | source)
XLA Modules:
  0.0 239.8 jit_solution(3080508734365883089)
XLA Ops:
  0.6 0.0 copy-start
  0.6 234.4 %muon_group.1 = (f32[4,32,8192]{2,1,0:T(8,128)S(1)}, bf16[4,32,8192]{2,1,0:T(8,128)(2,1)S(1)}) custom-call(f32[4,32,8192]{2,1,0:T(8,128)} %m_hbm.1, bf16[4,128,8192]{2,1,0:T(8,128)(2,1)} %bitcast.1), custom_call_target="tpu_custom_call" | custom-call | tf_op jit(solution)/shard_map/muon_group/pallas_call | solution.py:437
  235.1 0.0 copy-done
  235.1 2.7 %multiply_subtract_fusion = f32[4,32,8192]{2,1,0:T(8,128)} fusion(bf16[4,32,8192]{2,1,0:T(8,128)(2,1)S(1)} %get-tuple-element.4, f32[4,32,8192]{2,1,0:T(8,128)S(1)} %copy-done), kind=kLoop, calls=%fused_computation | loop fusion | flops 4194304 | bytes 10485760 | tf_op jit(solution)/shard_map/sub | solution.py:458
  237.8 2.0 copy.6
Async XLA Ops:
  0.6 234.5 %copy-start = (f32[4,32,8192]{2,1,0:T(8,128)S(1)}, f32[4,32,8192]{2,1,0:T(8,128)}, u32[]{:S(2)}) copy-start(f32[4,32,8192]{2,1,0:T(8,128)} %param.3) | copy-start | bytes 12582916

commit v9 on v5

--- a/solution.py
+++ b/solution.py
@@ -29,7 +29,7 @@
 
 def muon_kernel(m_hbm, g_hbm, mnew_hbm, xfin_hbm,
                 gown, grecv, relay, mbuf, x0, xrow, xfull,
-                nown, npair, nall, part, drecv, red, comb, rsrecv, agbuf, amat, bmat,
+                nown, npair, nall, part, drecv, red, rsrecv, agbuf, amat, bmat,
                 cmid, chold1, chold2, bmid, bhold1, bhold2,
                 load_sem, out_sem, gsend, grcv, nsend, nrcv, csend, cmsem, ch1sem, ch2sem, cfsem,
                 bsend, bmsem, bh1sem, bh2sem, bfsem,
@@ -283,22 +283,14 @@
     bcol = min(256, quarter)
 
     near_x, near_y, diagonal = (pos_of(*c) for c in square)
-    to_x, to_y = {'fsdp': fx}, {'dp': fy}
-    sub = chunk // 2
-
-    def sub_ds(pos, h):
-        return pl.ds(pl.multiple_of(pos * chunk + h * sub, sub), sub)
-
     def pair_of(it, n):
         cs = chunk_ds((diagonal, near_x, near_y, my_pos)[n])
         return remote(part.at[it, 1 - t, cs, :], drecv.at[it, cs, :], dsend.at[it, n], drcv.at[it, n], partner)
 
     def reduce_of(it, n):
-        src = (red.at[it, sub_ds(diagonal, 0), :], red.at[it, sub_ds(diagonal, 1), :],
-               red.at[it, sub_ds(near_x, 0), :], red.at[it, sub_ds(near_y, 1), :],
-               comb.at[it, 0], comb.at[it, 1])[n]
-        to = (to_x, to_y, to_x, to_y, to_y, to_x)[n]
-        return remote(src, rsrecv.at[it, n], rssend.at[it, n], rsrcv.at[it, n], to)
+        py, px = square[(2, 0, 1)[n]]
+        return remote(red.at[it, chunk_ds(pos_of(py, px)), :], rsrecv.at[it, n], rssend.at[it, n], rsrcv.at[it, n],
+                      {'dp': py, 'fsdp': px})
 
     def gather_of(it, n):
         mine = agbuf.at[it, packed_ds(t, my_pos), :]
@@ -314,9 +306,8 @@
         for n in range(4):
             pair_of(it, n).wait_send()
             forward_of(it, n).wait_send()
-        for n in range(6):
+        for n in range(3):
             reduce_of(it, n).wait_send()
-        for n in range(3):
             gather_of(it, n).wait_send()
 
     def half_gram(it, h):
@@ -339,25 +330,17 @@
             pair_of(it, n).wait_recv()
             cs = chunk_ds(pos)
             red[it, cs, :] = part[it, t, cs, :] + drecv[it, cs, :]
-            for m in ((0, 1), (2,), (3,), ())[n]:
-                reduce_of(it, m).start()
-        reduce_of(it, 0).wait_recv()
-        comb[it, 0] = red[it, sub_ds(near_y, 0), :] + rsrecv[it, 0]
-        reduce_of(it, 4).start()
-        reduce_of(it, 1).wait_recv()
-        comb[it, 1] = red[it, sub_ds(near_x, 1), :] + rsrecv[it, 1]
-        reduce_of(it, 5).start()
+            if n < 3:
+                reduce_of(it, n).start()
 
         @pl.when(it > 0)
         def _():
             drain(it - 1)
 
-        for h in range(2):
-            reduce_of(it, 2 + h).wait_recv()
-            reduce_of(it, 4 + h).wait_recv()
-            total = (red[it, sub_ds(my_pos, h), :] + rsrecv[it, 2 + h]) + rsrecv[it, 4 + h]
-            mine = pl.ds(pl.multiple_of(t * (HALF * BLK) + my_pos * chunk + h * sub, sub), sub)
-            agbuf[it, mine, :] = total.astype(BF16)
+        for n in (1, 2, 0):
+            reduce_of(it, n).wait_recv()
+        total = (red[it, chunk_ds(my_pos), :] + rsrecv[it, 1]) + (rsrecv[it, 2] + rsrecv[it, 0])
+        agbuf[it, packed_ds(t, my_pos), :] = total.astype(BF16)
         for n in (2, 0, 1):
             gather_of(it, n).start()
         forward_of(it, 0).start()
@@ -424,15 +407,14 @@
         pltpu.VMEM((NS_STEPS, 2, packed // 2, BLK), F32),
         pltpu.VMEM((NS_STEPS, packed // 2, BLK), F32),
         pltpu.VMEM((NS_STEPS, packed // 2, BLK), F32),
-        pltpu.VMEM((NS_STEPS, 2, chunk // 2, BLK), F32),
-        pltpu.VMEM((NS_STEPS, 6, chunk // 2, BLK), F32),
+        pltpu.VMEM((NS_STEPS, 3, chunk, BLK), F32),
         pltpu.VMEM((NS_STEPS, packed, BLK), BF16),
         pltpu.VMEM((all_rows, all_rows), BF16),
         pltpu.VMEM((all_rows, all_rows), BF16),
         *relays, *relays,
         dma((2, n_mat)), dma((n_mat,)), dma((n_mat, 6)), dma((n_mat, 6)),
         dma((n_oth + 1,)), dma((n_oth + 1,)), *relay_sems, *relay_sems,
-        dma((NS_STEPS, 4)), dma((NS_STEPS, 4)), dma((NS_STEPS, 6)), dma((NS_STEPS, 6)),
+        dma((NS_STEPS, 4)), dma((NS_STEPS, 4)), dma((NS_STEPS, 3)), dma((NS_STEPS, 3)),
         dma((NS_STEPS, 3)), dma((NS_STEPS, 3)), dma((NS_STEPS, 4)), dma((NS_STEPS, 4)), pltpu.SemaphoreType.REGULAR((3,)),
     ]
     anyspace = pl.BlockSpec(memory_space=pl.ANY)

time: 239 us -> 234 us (0.979)
  Pallas kernels: 233 us -> 229 us
    pallas_call x1, Pallas kernels: 233 us -> 229 us  [run_kernel(): pl.pallas_call(muon_kernel, out_shape=(jax.ShapeDtypeStruct(m_blk.shape,...]
where the time goes in v9:
time: 234 us
  Pallas kernels  229 us (98%)
  other arithmetic  2.67 us (1%)
    pallas_call x1, Pallas kernels, run_kernel(): pl.pallas_call(muon_kernel, out_shape=(jax.ShapeDtypeStruct(m_blk.shape,...  229 us

profile of v9, /device:TPU:97, one launch (start us, length us, event | category | flops | bytes accessed | tf_op | source)
XLA Modules:
  0.0 234.3 jit_solution(4202215978948011340)
XLA Ops:
  0.6 0.0 copy-start
  0.6 228.9 %muon_group.1 = (f32[4,32,8192]{2,1,0:T(8,128)S(1)}, bf16[4,32,8192]{2,1,0:T(8,128)(2,1)S(1)}) custom-call(f32[4,32,8192]{2,1,0:T(8,128)} %m_hbm.1, bf16[4,128,8192]{2,1,0:T(8,128)(2,1)} %bitcast.1), custom_call_target="tpu_custom_call" | custom-call | tf_op jit(solution)/shard_map/muon_group/pallas_call | solution.py:421
  229.6 0.0 copy-done
  229.6 2.7 %multiply_subtract_fusion = f32[4,32,8192]{2,1,0:T(8,128)} fusion(bf16[4,32,8192]{2,1,0:T(8,128)(2,1)S(1)} %get-tuple-element.4, f32[4,32,8192]{2,1,0:T(8,128)S(1)} %copy-done), kind=kLoop, calls=%fused_computation | loop fusion | flops 4194304 | bytes 10485760 | tf_op jit(solution)/shard_map/sub | solution.py:442
  232.3 2.0 copy.6
Async XLA Ops:
  0.6 229.0 %copy-start = (f32[4,32,8192]{2,1,0:T(8,128)S(1)}, f32[4,32,8192]{2,1,0:T(8,128)}, u32[]{:S(2)}) copy-start(f32[4,32,8192]{2,1,0:T(8,128)} %param.3) | copy-start | bytes 12582916

commit v10 on v9

--- a/solution.py
+++ b/solution.py
@@ -22,8 +22,8 @@
 VMEM_MIB = 47
 SIDE = 4
 BLK = 128
-TRI = ((0, 0), (0, 1), (1, 1), (0, 2), (0, 3), (2, 2), (2, 3), (3, 3), (1, 2), (1, 3))
-HALF = len(TRI) // 2
+SUB = BLK // 2
+HALF_ROWS = 3 * BLK + 3 * SUB
 PLACE = ((0, 1), (1, 0), (1, 1), (0, 0))
 
 
@@ -272,13 +272,13 @@
 
     fy, fx = y + 1 - 2 * (y % 2), x + 1 - 2 * (x % 2)
     square = ((y, fx), (fy, x), (fy, fx))
-    chunk = HALF * BLK // 4
+    chunk = HALF_ROWS // 4
 
     def chunk_ds(pos):
         return pl.ds(pl.multiple_of(pos * chunk, chunk), chunk)
 
     def packed_ds(core, pos):
-        return pl.ds(pl.multiple_of(core * (HALF * BLK) + pos * chunk, chunk), chunk)
+        return pl.ds(pl.multiple_of(core * HALF_ROWS + pos * chunk, chunk), chunk)
 
     bcol = min(256, quarter)
 
@@ -316,10 +316,30 @@
         square_gram = lax.dot_general(pair_rows, pair_rows, nt, preferred_element_type=F32)
         cross_gram = lax.dot_general(xfull[pl.ds(pl.multiple_of(h * BLK, BLK), BLK), :], xfull[2 * BLK:, :], nt,
                                      preferred_element_type=F32)
-        blocks = (square_gram[:BLK, :BLK], square_gram[:BLK, BLK:], square_gram[BLK:, BLK:],
-                  cross_gram[:, :BLK], cross_gram[:, BLK:])
-        for n, block in enumerate(blocks):
-            part[it, h, n * BLK:(n + 1) * BLK, :] = block
+        corners = jnp.where(left_lanes, pltpu.roll(square_gram[BLK + SUB:, BLK:], SUB, 1), square_gram[SUB:BLK, :BLK])
+        rows_of = (square_gram[:BLK, BLK:], cross_gram[:, :BLK], cross_gram[:, BLK:],
+                   square_gram[:SUB, :BLK], square_gram[BLK:BLK + SUB, BLK:], corners)
+        at = 0
+        for block in rows_of:
+            part[it, h, at:at + block.shape[0], :] = block
+            at += block.shape[0]
+
+    left_lanes = lax.broadcasted_iota(jnp.int32, (SUB, BLK), 1) < SUB
+
+    def assemble(it, h):
+        base = h * HALF_ROWS
+        for n, (bi, bj) in enumerate(((2 * h, 2 * h + 1), (h, 2), (h, 3))):
+            block = agbuf[it, base + n * BLK:base + (n + 1) * BLK, :]
+            amat[bi * BLK:(bi + 1) * BLK, bj * BLK:(bj + 1) * BLK] = block
+            amat[bj * BLK:(bj + 1) * BLK, bi * BLK:(bi + 1) * BLK] = block.astype(F32).T.astype(BF16)
+        base += 3 * BLK
+        corners = agbuf[it, base + 2 * SUB:base + 3 * SUB, :].astype(F32)
+        for n, corner in enumerate((corners, pltpu.roll(corners, SUB, 1))):
+            lo_, mid_, hi_ = (2 * h + n) * BLK, (2 * h + n) * BLK + SUB, (2 * h + n + 1) * BLK
+            upper = agbuf[it, base + n * SUB:base + (n + 1) * SUB, :]
+            amat[lo_:mid_, lo_:hi_] = upper
+            flipped = jnp.concatenate([upper.astype(F32), corner], axis=0).T
+            amat[mid_:hi_, lo_:hi_] = jnp.where(left_lanes, flipped[SUB:, :], corner).astype(BF16)
 
     def iteration(it, carry):
         half_gram(it, 1 - t)
@@ -349,11 +369,8 @@
             forward_of(it, n + 1).start()
         for n in range(4):
             forward_of(it, n).wait_recv()
-        for n, (bi, bj) in enumerate(TRI):
-            block = agbuf[it, n * BLK:(n + 1) * BLK, :]
-            amat[bi * BLK:(bi + 1) * BLK, bj * BLK:(bj + 1) * BLK] = block
-            if bi != bj:
-                amat[bj * BLK:(bj + 1) * BLK, bi * BLK:(bi + 1) * BLK] = block.astype(F32).T.astype(BF16)
+        assemble(it, 0)
+        assemble(it, 1)
         for bi in range(2):
             rs = slice(2 * BLK * bi, 2 * BLK * (bi + 1))
             sq = jnp.dot(amat[rs, :], amat[...], preferred_element_type=F32).astype(BF16)
@@ -382,7 +399,7 @@
     n_mat, rows, cols = m_blk.shape
     all_rows = rows * SIDE * SIDE
     quarter = cols // SIDE
-    packed = len(TRI) * BLK
+    packed = 2 * HALF_ROWS
     chunk = packed // 8
     n_oth = SIDE * SIDE - 1
     dma = pltpu.SemaphoreType.DMA

time: 234 us -> 233 us (level)
  no operation moved by 1% of the time
where the time goes in v10:
time: 233 us
  Pallas kernels  227 us (97%)
  other arithmetic  2.67 us (1%)
    pallas_call x1, Pallas kernels, run_kernel(): pl.pallas_call(muon_kernel, out_shape=(jax.ShapeDtypeStruct(m_blk.shape,...  227 us

profile of v10, /device:TPU:97, one launch (start us, length us, event | category | flops | bytes accessed | tf_op | source)
XLA Modules:
  0.0 232.7 jit_solution(1347904951638522113)
XLA Ops:
  0.6 0.0 copy-start
  0.6 227.3 %muon_group.1 = (f32[4,32,8192]{2,1,0:T(8,128)S(1)}, bf16[4,32,8192]{2,1,0:T(8,128)(2,1)S(1)}) custom-call(f32[4,32,8192]{2,1,0:T(8,128)} %m_hbm.1, bf16[4,128,8192]{2,1,0:T(8,128)(2,1)} %bitcast.1), custom_call_target="tpu_custom_call" | custom-call | tf_op jit(solution)/shard_map/muon_group/pallas_call | solution.py:438
  228.0 0.0 copy-done
  228.0 2.7 %multiply_subtract_fusion = f32[4,32,8192]{2,1,0:T(8,128)} fusion(bf16[4,32,8192]{2,1,0:T(8,128)(2,1)S(1)} %get-tuple-element.4, f32[4,32,8192]{2,1,0:T(8,128)S(1)} %copy-done), kind=kLoop, calls=%fused_computation | loop fusion | flops 4194304 | bytes 10485760 | tf_op jit(solution)/shard_map/sub | solution.py:459
  230.7 2.0 copy.6
Async XLA Ops:
  0.6 227.4 %copy-start = (f32[4,32,8192]{2,1,0:T(8,128)S(1)}, f32[4,32,8192]{2,1,0:T(8,128)}, u32[]{:S(2)}) copy-start(f32[4,32,8192]{2,1,0:T(8,128)} %param.3) | copy-start | bytes 12582916
